TPU v7x, 8 devices: a whole 2x2x1 slice. The times are simulated.
8 devices in a mesh: dp: 1 (over z), ey: 2 (over y), ex: 2 (over x), ec: 2 (over core).
Axes of the slice: x: 2, y: 2, z: 1, core: 2. Of those that a mesh axis runs over, the one named last changes fastest.
Arguments:
- x: bfloat16 [2048, 2048], P(('dp', 'ey', 'ex', 'ec'))
- ids: int32 [2048, 6], P(('dp', 'ey', 'ex', 'ec'))
- gates: float32 [2048, 6], P(('dp', 'ey', 'ex', 'ec'))
- w1: bfloat16 [64, 2048, 1408], P(('ey', 'ex', 'ec'))
- w3: bfloat16 [64, 2048, 1408], P(('ey', 'ex', 'ec'))
- w2: bfloat16 [64, 1408, 2048], P(('ey', 'ex', 'ec'))
- ws1: bfloat16 [2048, 2816], replicated
- ws3: bfloat16 [2048, 2816], replicated
- ws2: bfloat16 [2816, 2048], replicated
Outputs:
- output: bfloat16 [2048, 2048], P(('dp', 'ey', 'ex', 'ec'))
All inputs are finite; a program needn't handle non-finite values.
Results may differ from a plain program's by a relative error of at most 0.00579921.
Values are sent between devices in bfloat16 or wider.
A program may use at most 1 GiB of HBM per device.

v0:
```python
import jax
import jax.numpy as jnp
from jax import lax
from jax.sharding import PartitionSpec as P

EXP = ("ey", "ex", "ec")
ALL = ("dp", "ey", "ex", "ec")


def solution(mesh):
    pg = mesh.shape["ey"] * mesh.shape["ex"] * mesh.shape["ec"]

    def local(x, ids, gates, w1, w3, w2, ws1, ws3, ws2):
        t, hd = x.shape
        top = ids.shape[1]
        el = w1.shape[0]
        ne = el * pg
        cap = min(t, 2 * ((t * top + ne - 1) // ne))
        m = t * top
        hit = ids[:, :, None] == jnp.arange(ne)[None, None, :]
        c = jnp.any(hit, axis=1)
        tri = (jnp.arange(t)[None, :] < jnp.arange(t)[:, None]).astype(jnp.bfloat16)
        cnt = jnp.dot(tri, c.astype(jnp.bfloat16), preferred_element_type=jnp.float32).astype(jnp.int32)
        rank = jnp.sum(jnp.where(hit, cnt[:, None, :], 0), axis=2)
        pos = (ids * cap + rank).reshape(m)
        sel = (cnt.T[:, None, :] == jnp.arange(cap)[None, :, None]) & c.T[:, None, :]
        disp = sel.astype(jnp.bfloat16).reshape(ne * cap, t)
        send = jnp.dot(disp, x, preferred_element_type=jnp.float32).astype(x.dtype)
        recv = lax.all_to_all(send, EXP, 0, 0, tiled=True)
        recv = recv.reshape(pg, el, cap, hd).transpose(1, 0, 2, 3).reshape(el, pg * cap, hd)
        a = jnp.einsum("erh,ehf->erf", recv, w1, preferred_element_type=jnp.float32)
        b = jnp.einsum("erh,ehf->erf", recv, w3, preferred_element_type=jnp.float32)
        hid = (jax.nn.silu(a) * b).astype(jnp.bfloat16)
        out = jnp.einsum("erf,efh->erh", hid, w2, preferred_element_type=jnp.float32).astype(jnp.bfloat16)
        out = out.reshape(el, pg, cap, hd).transpose(1, 0, 2, 3).reshape(pg * el * cap, hd)
        back = lax.all_to_all(out, EXP, 0, 0, tiled=True)
        got = back[pos].reshape(t, top, hd)
        moe = jnp.sum(gates[:, :, None] * got.astype(jnp.float32), axis=1)
        sa = jnp.dot(x, ws1, preferred_element_type=jnp.float32)
        sb = jnp.dot(x, ws3, preferred_element_type=jnp.float32)
        sh = (jax.nn.silu(sa) * sb).astype(jnp.bfloat16)
        s = jnp.dot(sh, ws2, preferred_element_type=jnp.float32).astype(jnp.bfloat16)
        return (x.astype(jnp.float32) + s.astype(jnp.float32) + moe).astype(jnp.bfloat16)

    return jax.shard_map(local, mesh=mesh,
                         in_specs=(P(ALL), P(ALL), P(ALL), P(EXP), P(EXP), P(EXP), P(), P(), P()),
                         out_specs=P(ALL), check_vma=False)
```

profile of v0, /device:TPU:0, one launch (start us, length us, event | category | flops | bytes accessed | tf_op | source)
XLA Modules:
  0.0 447.5 jit_solution(13073307370384495004)
XLA Ops:
  0.0 0.7 fusion.6
  0.8 0.2 convolution_convert_fusion.3
  1.0 0.1 eq.39
  1.0 1.5 fusion.1
  2.5 4.9 %convolution_convert_fusion = bf16[3072,2048]{1,0:T(8,128)(2,1)S(1)} fusion(pred[3072,256]{1,0:T(32,128)(4,1)} %fusion.1, bf16[256,2048]{1,0:T(8,128)(2,1)} %param.9), kind=kOutput, calls=%fused_computation.3 | convolution fusion | flops 3227516928 | bytes 14417920 | tf_op jit(solution)/shard_map/dot_general | solution.py:28
  7.4 143.0 %all_to_all.21 = bf16[8,384,2048]{2,1,0:T(8,128)(2,1)S(1)} all-to-all(bf16[8,384,2048]{2,1,0:T(8,128)(2,1)S(1)} %bitcast.47), channel_id=1, replica_groups=mesh['dp'=1,'ey'=2,'ex'=2,'ec'=2] {'ey','ex','ec'}, dimensions={0} | all-to-all | bytes 25165824 | tf_op jit(solution)/shard_map/all_to_all | solution.py:29
  150.5 5.0 %copy.23 = bf16[8,8,48,2048]{3,2,0,1:T(8,128)(2,1)} copy(bf16[8,8,48,2048]{3,2,1,0:T(8,128)(2,1)S(1)} %bitcast.49) | data formatting | bytes 25165824 | tf_op jit(solution)/shard_map/reshape | solution.py:30
  155.5 32.1 %fusion.10 = f32[8,384,1408]{2,1,0:T(8,128)} fusion(bf16[8,384,2048]{2,1,0:T(8,128)(2,1)} %bitcast.50, bf16[8,2048,1408]{2,1,0:T(8,128)(2,1)} %param.12), kind=kOutput, calls=%fused_computation.25 | convolution fusion | flops 17716740096 | bytes 76021760 | tf_op jit(solution)/shard_map/erh,ehf->erf/dot_general | solution.py:31
  187.6 50.3 %convolution_convert_fusion.1 = bf16[8,384,2048]{2,1,0:T(8,128)(2,1)} fusion(bf16[8,1408,2048]{2,1,0:T(8,128)(2,1)} %param.14, f32[8,384,1408]{2,1,0:T(8,128)} %fusion.10, bf16[8,384,2048]{2,1,0:T(8,128)(2,1)} %bitcast.51, bf16[8,2048,1408]{2,1,0:T(8,128)(2,1)} %param.13), kind=kOutput, calls=%fused_computation.4 | convolution fusion | flops 35465723904 | bytes 134742016 | tf_op jit(solution)/shard_map/erf,efh->erh/dot_general | solution.py:34
  237.9 10.7 %copy.24 = bf16[8,8,48,2048]{3,2,0,1:T(8,128)(2,1)} copy(bf16[8,8,48,2048]{3,2,1,0:T(8,128)(2,1)} %bitcast.52) | data formatting | bytes 25165824 | tf_op jit(solution)/shard_map/reshape | solution.py:35
  248.6 0.0 copy-start.1
  248.6 0.0 copy-start.2
  248.6 0.0 copy-start
  248.6 4.4 all-to-all-start.1
  253.0 0.0 copy-done.1
  253.0 0.1 select_reduce_fusion
  253.1 0.1 copy.25
  253.2 0.1 reshape.62
  253.4 0.0 copy-done.2
  253.4 0.1 copy.22
  253.6 0.0 copy-done
  253.6 9.1 %fusion.9 = f32[256,2816]{1,0:T(8,128)} fusion(bf16[256,2048]{1,0:T(8,128)(2,1)S(1)} %copy-done, bf16[2048,2816]{1,0:T(8,128)(2,1)} %param.15), kind=kOutput, calls=%fused_computation.24 | convolution fusion | flops 2952790016 | bytes 15466496 | tf_op jit(solution)/shard_map/dot_general | solution.py:39
  262.7 129.1 %all-to-all-done.1 = bf16[8,384,2048]{2,1,0:T(8,128)(2,1)} async-done(((bf16[8,384,2048]{2,1,0:T(8,128)(2,1)}), bf16[8,384,2048]{2,1,0:T(8,128)(2,1)}, u32[]{:S(2)}, u32[]{:S(2)}) %all-to-all-start.1) | async-done | bytes 12582944 | tf_op jit(solution)/shard_map/all_to_all | solution.py:36
  391.8 18.9 %gather_fusion = bf16[1536,2048]{1,0:T(8,128)(2,1)} fusion(bf16[3072,2048]{1,0:T(8,128)(2,1)} %bitcast.12, s32[2048]{0:T(1024)S(1)} %pad_clamp_fusion), kind=kCustom, calls=%fused_computation | custom fusion | bytes 12589056 | tf_op jit(solution)/shard_map/gather | solution.py:37
  410.7 11.7 %reshape.63 = f32[256,6,2048]{2,1,0:T(8,128)} reshape(bf16[1536,2048]{1,0:T(8,128)(2,1)} %gather_fusion) | data formatting | bytes 18874368 | tf_op jit(solution)/shard_map/convert_element_type | solution.py:38
  422.4 9.5 %multiply_reduce_fusion = f32[256,2048]{1,0:T(8,128)S(1)} fusion(f32[256,6,2048]{2,1,0:T(8,128)} %reshape.63, f32[256,6]{1,0:T(8,128)S(1)} %copy.22), kind=kLoop, calls=%fused_computation.2 | loop fusion | flops 5767168 | bytes 14686208 | tf_op jit(solution)/shard_map/reduce_sum | solution.py:38
  431.9 15.6 %fusion.5 = bf16[256,2048]{1,0:T(8,128)(2,1)} fusion(f32[256,2048]{1,0:T(8,128)S(1)} %multiply_reduce_fusion, bf16[2816,2048]{1,0:T(8,128)(2,1)} %param.17, bf16[256,2048]{1,0:T(8,128)(2,1)S(1)} %copy-done, bf16[2048,2816]{1,0:T(8,128)(2,1)} %param.16, f32[256,2816]{1,0:T(8,128)} %fusion.9), kind=kOutput, calls=%fused_computation.13 | convolution fusion | flops 5913051136 | bytes 30146560 | tf_op jit(solution)/shard_map/dot_general | solution.py:42
  (4 shorter events, 0.0 us)
Async XLA Ops:
  248.6 4.5 copy-start.1
  248.6 4.8 %copy-start.2 = (f32[256,6]{0,1:T(8,128)S(1)}, f32[256,6]{0,1:T(8,128)}, u32[]{:S(2)}) copy-start(f32[256,6]{0,1:T(8,128)} %param.11) | copy-start | bytes 18436
  248.6 5.0 %copy-start = (bf16[256,2048]{1,0:T(8,128)(2,1)S(1)}, bf16[256,2048]{1,0:T(8,128)(2,1)}, u32[]{:S(2)}) copy-start(bf16[256,2048]{1,0:T(8,128)(2,1)} %param.9) | copy-start | bytes 3145732
  248.6 143.2 %all-to-all-start.1 = ((bf16[8,384,2048]{2,1,0:T(8,128)(2,1)}), bf16[8,384,2048]{2,1,0:T(8,128)(2,1)}, u32[]{:S(2)}, u32[]{:S(2)}) async-start(bf16[8,384,2048]{2,1,0:T(8,128)(2,1)} %bitcast.48), calls=%async_computation.1 | async-start | bytes 25165824 | tf_op jit(solution)/shard_map/all_to_all | solution.py:36
where the time goes:
time: 448 us
  blocking collectives  143 us (32%)
  waiting for transfers between devices  129 us (29%)
  matrix products  112 us (25%)
  local copies, waits for them, and re-layouts  46.9 us (10%)
  other arithmetic  11.8 us (3%)
    all_to_all x1, blocking collectives, local(): recv = lax.all_to_all(send, EXP, 0, 0, tiled=True)  143 us
    all_to_all x1, waiting for transfers between devices, local(): back = lax.all_to_all(out, EXP, 0, 0, tiled=True)  129 us
    dot_general x1, matrix products, local(): jnp.einsum('erf,efh->erh', hid, w2, preferred_element_type=jnp.float32)  50.3 us
    dot_general x1, matrix products, local(): a = jnp.einsum('erh,ehf->erf', recv, w1, preferred_element_type=jnp.float32)  32.1 us
    gather x1, local copies, waits for them, and re-layouts, local(): got = back[pos].reshape(t, top, hd)  18.9 us
    dot_general x1, matrix products, local(): jnp.dot(sh, ws2, preferred_element_type=jnp.float32).astype(jnp.bfloat16)  15.6 us
    convert_element_type x1, local copies, waits for them, and re-layouts, local(): moe = jnp.sum(gates[:, :, None] * got.astype(jnp.float32), axis=1)  11.7 us
    reshape x1, local copies, waits for them, and re-layouts, local(): out.reshape(el, pg, cap, hd).transpose(1, 0, 2, 3)  10.7 us
  transfers between devices with their start and end apart: 1, of which 1 were waited for; matrix products, arithmetic and copies ran while one was open for 2% of the time, Pallas kernels for 0%

commit v1 on v0

v1 whole, which is shorter than its diff:
```python
import jax
import jax.numpy as jnp
from jax import lax
from jax.sharding import PartitionSpec as P

EXP = ("ey", "ex", "ec")
ALL = ("dp", "ey", "ex", "ec")


def split3(g):
    g1 = lax.reduce_precision(g, 8, 7)
    r = g - g1
    g2 = lax.reduce_precision(r, 8, 7)
    g3 = r - g2
    return [v.astype(jnp.bfloat16) for v in (g1, g2, g3)]


def solution(mesh):
    pg = mesh.shape["ey"] * mesh.shape["ex"] * mesh.shape["ec"]

    def local(x, ids, gates, w1, w3, w2, ws1, ws3, ws2):
        t, hd = x.shape
        top = ids.shape[1]
        el = w1.shape[0]
        ne = el * pg
        cap = min(t, 2 * ((t * top + ne - 1) // ne))
        me = lax.axis_index(EXP)
        xg = lax.all_gather(x, EXP, axis=0, tiled=True).reshape(pg, t, hd)
        idg = lax.all_gather(ids, EXP, axis=0, tiled=True).reshape(pg, t, top)
        gg = lax.all_gather(gates, EXP, axis=0, tiled=True).reshape(pg, t, top)
        mine = me * el + jnp.arange(el)
        hit = idg[:, :, :, None] == mine
        c = jnp.any(hit, axis=2)
        g = jnp.sum(jnp.where(hit, gg[:, :, :, None], 0.0), axis=2)
        tri = (jnp.arange(t)[None, :] < jnp.arange(t)[:, None]).astype(jnp.bfloat16)
        cnt = jnp.einsum("ab,sbe->sae", tri, c.astype(jnp.bfloat16), preferred_element_type=jnp.float32).astype(jnp.int32)
        sel = (cnt[:, :, :, None] == jnp.arange(cap)) & c[:, :, :, None]
        disp = sel.astype(jnp.bfloat16).reshape(pg, t, el * cap)
        rows = jnp.einsum("std,sth->sdh", disp, xg, preferred_element_type=jnp.float32).astype(jnp.bfloat16)
        recv = rows.reshape(pg, el, cap, hd).transpose(1, 0, 2, 3).reshape(el, pg * cap, hd)
        a = jnp.einsum("erh,ehf->erf", recv, w1, preferred_element_type=jnp.float32)
        b = jnp.einsum("erh,ehf->erf", recv, w3, preferred_element_type=jnp.float32)
        hid = (jax.nn.silu(a) * b).astype(jnp.bfloat16)
        out = jnp.einsum("erf,efh->erh", hid, w2, preferred_element_type=jnp.float32).astype(jnp.bfloat16)
        out = out.reshape(el, pg, cap, hd).transpose(1, 0, 2, 3).reshape(pg, el * cap, hd)
        wg = jnp.where(sel, g[:, :, :, None], 0.0).reshape(pg, t, el * cap)
        part = sum(jnp.einsum("std,sdh->sth", v, out, preferred_element_type=jnp.float32) for v in split3(wg))
        moe = lax.psum_scatter(part.reshape(pg * t, hd), EXP, scatter_dimension=0, tiled=True)
        sa = jnp.dot(x, ws1, preferred_element_type=jnp.float32)
        sb = jnp.dot(x, ws3, preferred_element_type=jnp.float32)
        sh = (jax.nn.silu(sa) * sb).astype(jnp.bfloat16)
        s = jnp.dot(sh, ws2, preferred_element_type=jnp.float32).astype(jnp.bfloat16)
        return (x.astype(jnp.float32) + s.astype(jnp.float32) + moe).astype(jnp.bfloat16)

    return jax.shard_map(local, mesh=mesh,
                         in_specs=(P(ALL), P(ALL), P(ALL), P(EXP), P(EXP), P(EXP), P(), P(), P()),
                         out_specs=P(ALL), check_vma=False)
```

time: 448 us -> 336 us (0.75)
  blocking collectives: 143 us -> 25.5 us
  matrix products: 112 us -> 153 us
  local copies, waits for them, and re-layouts: 46.9 us -> 18.3 us
  between operations: 0.12 us -> 13.5 us
  waiting for transfers between devices: 129 us -> 121 us
  other arithmetic: 11.8 us -> 4.16 us
    all_to_all x1 -> x0, blocking collectives: 143 us -> none  [local(): recv = lax.all_to_all(send, EXP, 0, 0, tiled=True)]
    all_to_all x1 -> x0, waiting for transfers between devices: 129 us -> none  [local(): back = lax.all_to_all(out, EXP, 0, 0, tiled=True)]
    reduce_scatter x0 -> x1, waiting for transfers between devices: none -> 96.9 us  [local(): lax.psum_scatter(part.reshape(pg * t, hd), EXP, scatter_dimension=0, tile...]
    dot_general x2 -> x5, matrix products: 5.09 us -> 45.2 us  [the longest x3 33.3 us: local(): jnp.einsum('std,sdh->sth', v, out, preferred_element_type=jnp.float32)]
    all_gather x0 -> x2, blocking collectives: none -> 25.5 us  [the longest x1 14.2 us: local(): idg = lax.all_gather(ids, EXP, axis=0, tiled=True).reshape(pg, t, top)]
    all_gather x0 -> x1, waiting for transfers between devices: none -> 23.7 us  [local(): xg = lax.all_gather(x, EXP, axis=0, tiled=True).reshape(pg, t, hd)]
    gather x1 -> x0, local copies, waits for them, and re-layouts: 18.9 us -> none  [local(): got = back[pos].reshape(t, top, hd)]
    transpose x0 -> x2, local copies, waits for them, and re-layouts: none -> 17 us  [the longest x1 10.8 us: local(): rows.reshape(pg, el, cap, hd).transpose(1, 0, 2, 3)]
  transfers between devices with their start and end apart: 1 -> 2, of which waited for: 1 -> 2; matrix products, arithmetic and copies ran while one was open for 2% -> 4% of each run, Pallas kernels for 0% -> 0%
where the time goes in v1:
time: 336 us
  matrix products  153 us (46%)
  waiting for transfers between devices  121 us (36%)
  blocking collectives  25.5 us (8%)
  local copies, waits for them, and re-layouts  18.3 us (5%)
  between operations  13.5 us (4%)
  other arithmetic  4.16 us (1%)
    reduce_scatter x1, waiting for transfers between devices, local(): lax.psum_scatter(part.reshape(pg * t, hd), EXP, scatter_dimension=0, tile...  96.9 us
    dot_general x1, matrix products, local(): jnp.einsum('erf,efh->erh', hid, w2, preferred_element_type=jnp.float32)  50.3 us
    dot_general x3, matrix products, local(): jnp.einsum('std,sdh->sth', v, out, preferred_element_type=jnp.float32)  33.3 us
    dot_general x1, matrix products, local(): a = jnp.einsum('erh,ehf->erf', recv, w1, preferred_element_type=jnp.float32)  32.1 us
    all_gather x1, waiting for transfers between devices, local(): xg = lax.all_gather(x, EXP, axis=0, tiled=True).reshape(pg, t, hd)  23.7 us
    dot_general x1, matrix products, local(): jnp.dot(sh, ws2, preferred_element_type=jnp.float32).astype(jnp.bfloat16)  16.2 us
    all_gather x1, blocking collectives, local(): idg = lax.all_gather(ids, EXP, axis=0, tiled=True).reshape(pg, t, top)  14.2 us
    dot_general x1, matrix products, local(): jnp.einsum('std,sth->sdh', disp, xg, preferred_element_type=jnp.float32)  11.6 us
  transfers between devices with their start and end apart: 2, of which 2 were waited for; matrix products, arithmetic and copies ran while one was open for 4% of the time, Pallas kernels for 0%

profile of v1, /device:TPU:0, one launch (start us, length us, event | category | flops | bytes accessed | tf_op | source)
XLA Modules:
  0.0 335.5 jit_solution(6922894298449514743)
XLA Ops:
  6.5 0.0 all-gather.2.cloned.1.call-start
  6.5 0.7 all-gather.2.cloned.1.call-update
  7.3 0.0 reduce-scatter.2.cloned.1.call-start
  7.3 0.1 eq.43
  7.4 14.2 %all_gather.9 = s32[2048,6]{0,1:T(8,128)S(1)} all-gather(s32[256,6]{0,1:T(8,128)} %param.10), channel_id=1, replica_groups=mesh['dp'=1,'ey'=2,'ex'=2,'ec'=2] {'ey','ex','ec'}, dimensions={0}, use_global_device_ids=true | all-gather | bytes 55296 | tf_op jit(solution)/shard_map/all_gather | solution.py:29
  21.6 0.1 compare_reduce_fusion
  21.7 0.2 fusion.7
  21.9 1.5 fusion.2
  23.4 11.3 %all_gather.10 = f32[2048,6]{0,1:T(8,128)S(1)} all-gather(f32[256,6]{0,1:T(8,128)} %param.11), channel_id=1, replica_groups=mesh['dp'=1,'ey'=2,'ex'=2,'ec'=2] {'ey','ex','ec'}, dimensions={0}, use_global_device_ids=true | all-gather | bytes 55296 | tf_op jit(solution)/shard_map/all_gather | solution.py:30
  34.8 0.1 fusion.8
  34.9 2.4 fusion.1
  37.3 23.7 %all-gather.2.cloned.1.call-done = bf16[2048,2048]{1,0:T(8,128)(2,1)} async-done(((bf16[256,2048]{1,0:T(8,128)(2,1)}), bf16[2048,2048]{1,0:T(8,128)(2,1)}) %all-gather.2.cloned.1.call-update) | async-done | bytes 8388624 | tf_op jit(solution)/shard_map/all_gather | solution.py:28
  61.0 11.6 %convolution_convert_fusion = bf16[8,384,2048]{2,1,0:T(8,128)(2,1)} fusion(pred[8,256,384]{1,2,0:T(32,128)(4,1)} %fusion.2, bf16[8,256,2048]{2,1,0:T(8,128)(2,1)} %bitcast.85), kind=kOutput, calls=%fused_computation.2 | convolution fusion | flops 3227516928 | bytes 21757952 | tf_op jit(solution)/shard_map/std,sth->sdh/dot_general | solution.py:39
  72.6 10.8 %copy.26 = bf16[8,8,48,2048]{3,2,1,0:T(8,128)(2,1)} copy(bf16[8,8,48,2048]{3,2,0,1:T(8,128)(2,1)} %bitcast.83) | data formatting | bytes 25165824 | tf_op jit(solution)/shard_map/transpose | solution.py:40
  83.4 32.1 %fusion.13 = f32[8,384,1408]{2,1,0:T(8,128)} fusion(bf16[8,384,2048]{2,1,0:T(8,128)(2,1)} %bitcast.86, bf16[8,2048,1408]{2,1,0:T(8,128)(2,1)} %param.12), kind=kOutput, calls=%fused_computation.29 | convolution fusion | flops 17716740096 | bytes 76021760 | tf_op jit(solution)/shard_map/erh,ehf->erf/dot_general | solution.py:41
  115.5 50.3 %convolution_convert_fusion.1 = bf16[8,384,2048]{2,1,0:T(8,128)(2,1)} fusion(bf16[8,1408,2048]{2,1,0:T(8,128)(2,1)} %param.14, f32[8,384,1408]{2,1,0:T(8,128)} %fusion.13, bf16[8,384,2048]{2,1,0:T(8,128)(2,1)} %bitcast.87, bf16[8,2048,1408]{2,1,0:T(8,128)(2,1)} %param.13), kind=kOutput, calls=%fused_computation.3 | convolution fusion | flops 35465723904 | bytes 134742016 | tf_op jit(solution)/shard_map/erf,efh->erh/dot_general | solution.py:44
  165.8 6.2 %copy.27 = bf16[8,8,48,2048]{3,2,1,0:T(8,128)(2,1)S(1)} copy(bf16[8,8,48,2048]{3,2,0,1:T(8,128)(2,1)} %bitcast.88) | data formatting | bytes 25165824 | tf_op jit(solution)/shard_map/transpose | solution.py:45
  172.0 8.1 %fusion.15 = f32[8,256,2048]{2,1,0:T(8,128)} fusion(bf16[8,256,384]{1,2,0:T(8,128)(2,1)S(1)} %get-tuple-element.6, bf16[8,384,2048]{2,1,0:T(8,128)(2,1)S(1)} %bitcast.80), kind=kOutput, calls=%fused_computation.31 | convolution fusion | flops 3221225472 | bytes 30932992 | tf_op jit(solution)/shard_map/std,sdh->sth/dot_general | solution.py:47
  180.2 0.0 copy-start
  180.2 8.1 %fusion.14 = f32[8,256,2048]{2,1,0:T(8,128)} fusion(bf16[8,256,384]{1,2,0:T(8,128)(2,1)S(1)} %get-tuple-element.7, bf16[8,384,2048]{2,1,0:T(8,128)(2,1)S(1)} %bitcast.81), kind=kOutput, calls=%fused_computation.30 | convolution fusion | flops 3221225472 | bytes 30932992 | tf_op jit(solution)/shard_map/std,sdh->sth/dot_general | solution.py:47
  188.3 0.0 copy-done
  188.3 17.1 %add_add_fusion = f32[8,256,2048]{2,1,0:T(8,128)} fusion(f32[8,256,2048]{2,1,0:T(8,128)} %fusion.14, f32[8,256,2048]{2,1,0:T(8,128)} %fusion.15, bf16[8,256,384]{1,2,0:T(8,128)(2,1)S(1)} %copy-done, bf16[8,384,2048]{2,1,0:T(8,128)(2,1)S(1)} %bitcast.82), kind=kOutput, calls=%fused_computation.1 | convolution fusion | flops 3229614080 | bytes 64487424 | tf_op jit(solution)/shard_map/std,sdh->sth/dot_general | solution.py:47
  205.4 0.0 copy-start.1
  205.4 0.0 reduce-scatter.2.cloned.1.call-update
  205.4 1.2 copy-done.1
  206.6 9.0 %fusion.12 = f32[256,2816]{1,0:T(8,128)} fusion(bf16[256,2048]{1,0:T(8,128)(2,1)S(1)} %copy-done.1, bf16[2048,2816]{1,0:T(8,128)(2,1)} %param.15), kind=kOutput, calls=%fused_computation.28 | convolution fusion | flops 2952790016 | bytes 15466496 | tf_op jit(solution)/shard_map/dot_general | solution.py:49
  215.6 96.9 %reduce-scatter.2.cloned.1.call-done = f32[256,2048]{1,0:T(8,128)} async-done(((f32[2048,2048]{1,0:T(8,128)}), f32[256,2048]{1,0:T(8,128)}) %reduce-scatter.2.cloned.1.call-update) | async-done | bytes 2097168 | tf_op jit(solution)/shard_map/reduce_scatter | solution.py:48
  312.5 16.2 %fusion.6 = bf16[256,2048]{1,0:T(8,128)(2,1)} fusion(f32[256,2048]{1,0:T(8,128)} %reduce-scatter.2.cloned.1.call-done, bf16[2816,2048]{1,0:T(8,128)(2,1)} %param.17, bf16[256,2048]{1,0:T(8,128)(2,1)S(1)} %copy-done.1, bf16[2048,2816]{1,0:T(8,128)(2,1)} %param.16, f32[256,2816]{1,0:T(8,128)} %fusion.12), kind=kOutput, calls=%fused_computation.18 | convolution fusion | flops 5913051136 | bytes 30146560 | tf_op jit(solution)/shard_map/dot_general | solution.py:52
  (2 shorter events, 0.0 us)
Async XLA Ops:
  6.5 54.4 %all-gather.2.cloned.1.call-start = ((), (), s32[]{:S(2)}) async-start(), calls=%async_computation.1 | async-start | bytes 9437184 | tf_op jit(solution)/shard_map/all_gather | solution.py:28
  7.3 305.2 %reduce-scatter.2.cloned.1.call-start = ((), (), s32[]{:S(2)}) async-start(), calls=%async_computation.2 | async-start | bytes 18874368 | tf_op jit(solution)/shard_map/reduce_scatter | solution.py:48
  180.2 8.1 %copy-start = (bf16[8,256,384]{1,2,0:T(8,128)(2,1)S(1)}, bf16[8,256,384]{1,2,0:T(8,128)(2,1)}, u32[]{:S(2)}) copy-start(bf16[8,256,384]{1,2,0:T(8,128)(2,1)} %get-tuple-element.5) | copy-start | bytes 4718596
  205.4 1.2 copy-start.1
Sparse Core Ops, SparseCore 0:
  9.1 51.7 all-gather.1
  205.5 106.9 reduce-scatter.1

commit v2 on v0

v2 whole, which is shorter than its diff:
```python
import functools

import jax
import jax.numpy as jnp
from jax import lax
from jax.experimental import pallas as pl
from jax.experimental.pallas import tpu as pltpu
from jax.sharding import PartitionSpec as P

EXP = ("ey", "ex", "ec")
ALL = ("dp", "ey", "ex", "ec")
MESH = pl.DeviceIdType.MESH
ANY = pl.BlockSpec(memory_space=pl.ANY)
VM = pl.BlockSpec(memory_space=pltpu.VMEM)
BF = jnp.bfloat16
F32 = jnp.float32
VLIM = 67043328

NK = 4
NS = 3
CW = 256
NW = 4


def place():
    ey, ex, ec = (lax.axis_index(a) for a in EXP)
    dev = {"x": dict(ey=ey, ex=1 - ex, ec=ec), "y": dict(ey=1 - ey, ex=ex, ec=ec), "p": dict(ey=ey, ex=ex, ec=1 - ec)}
    chip = {"o": ey * 2 + ex, "x": ey * 2 + 1 - ex, "y": (1 - ey) * 2 + ex, "d": (1 - ey) * 2 + 1 - ex}
    return ey, ex, ec, dev, chip


def silu_mul(a, b):
    return (a * jax.nn.sigmoid(a) * b).astype(BF)


def first(el, cap, ids_ref, gates_ref, x_ref, w1_ref, w3_ref, ws1_ref, ws3_ref, h_ref, sh_ref, wc_ref,
          xg, acc, wb, disp, xe, hst, wst, mout, meta,
          xsem, wsem, osem, csem, msend, mrecv, ssem, rsem):
    ey, ex, ec, dev, chip = place()
    t = x_ref.shape[0]
    kw = x_ref.shape[1] // NK
    f = w1_ref.shape[2]
    half = t // 2
    lo, hi, full = pl.ds(0, half), pl.ds(half, half), pl.ds(0, t)
    mine = {c: ec * 4 + chip[c] for c in "oxyd"}
    theirs = {c: (1 - ec) * 4 + chip[c] for c in "oxyd"}
    nsh = 2 * NK
    nb = nsh + NK * el

    def block(b, go):
        slot = lax.rem(b, NS)

        @pl.when(b < nsh)
        def _():
            rows = pl.ds(pl.multiple_of(lax.rem(b, NK) * kw, kw), kw)
            cols = pl.ds(pl.multiple_of((b // NK) * f, 128), f)
            for i, w in enumerate((ws1_ref, ws3_ref)):
                go(pltpu.make_async_copy(w.at[rows, cols], wb.at[slot, :, pl.ds(i * f, f)], wsem.at[slot, i]))

        @pl.when((b >= nsh) & (b < nb))
        def _():
            q = b - nsh
            rows = pl.ds(pl.multiple_of((q // el) * kw, kw), kw)
            for i, w in enumerate((w1_ref, w3_ref)):
                go(pltpu.make_async_copy(w.at[lax.rem(q, el), rows], wb.at[slot, :, pl.ds(i * f, f)], wsem.at[slot, i]))

    def fetch(b):
        block(b, lambda c: c.start())

    def ready(b):
        block(b, lambda c: c.wait())

    for b in range(NS - 1):
        fetch(b)
    for k in range(NK):
        pltpu.make_async_copy(x_ref.at[:, pl.ds(k * kw, kw)], xg.at[k, mine["o"]], xsem.at[k]).start()

    ne = el * 8
    row = lax.broadcasted_iota(jnp.int32, (ne, t), 0)
    chosen = jnp.zeros((ne, t), F32)
    gate = jnp.zeros((ne, t), F32)
    for j in range(6):
        hit = ids_ref[j:j + 1, :] == row
        chosen = jnp.where(hit, 1.0, chosen)
        gate = jnp.where(hit, gates_ref[j:j + 1, :], gate)
    before = (lax.broadcasted_iota(jnp.int32, (t, t), 0) < lax.broadcasted_iota(jnp.int32, (t, t), 1))
    rank = jnp.dot(chosen.astype(BF), before.astype(F32).astype(BF), preferred_element_type=F32)
    rank = jnp.where(chosen > 0.0, rank, -1.0)
    for d in range(8):
        mout[d, 0:el, :] = rank[d * el:(d + 1) * el]
        mout[d, el:2 * el, :] = gate[d * el:(d + 1) * el]

    barrier = pltpu.get_barrier_semaphore()
    others = [(a, b, c) for a in (0, 1) for b in (0, 1) for c in (0, 1) if a + b + c]

    def flip(o):
        return [lax.rem(v + s, 2) for v, s in zip((ey, ex, ec), o)]

    for o in others:
        y2, x2, c2 = flip(o)
        pl.semaphore_signal(barrier, inc=1, device_id=dict(ey=y2, ex=x2, ec=c2), device_id_type=MESH)
    pl.semaphore_wait(barrier, len(others))

    for k in range(NK):
        pltpu.make_async_copy(x_ref.at[:, pl.ds(k * kw, kw)], xg.at[k, mine["o"]], xsem.at[k]).wait()

    def remote(k, src, rows, chan, to):
        ref = xg.at[k, src, rows]
        return pltpu.make_async_remote_copy(ref, ref, ssem.at[k, chan], rsem.at[k, chan], device_id=dev[to],
                                            device_id_type=MESH)

    def direct(k):
        for chan, to in enumerate("xyp"):
            remote(k, mine["o"], full, chan, to).start()

    def relay(k):
        remote(k, mine["x"], full, 0, "x").wait_recv()
        remote(k, mine["x"], lo, 3, "y").start()
        remote(k, mine["x"], full, 5, "p").start()
        remote(k, mine["y"], full, 1, "y").wait_recv()
        remote(k, mine["y"], hi, 4, "x").start()
        remote(k, mine["y"], full, 6, "p").start()

    def corner(k):
        remote(k, mine["d"], lo, 3, "y").wait_recv()
        remote(k, mine["d"], lo, 7, "p").start()
        remote(k, mine["d"], hi, 4, "x").wait_recv()
        remote(k, mine["d"], hi, 8, "p").start()

    def arrived(k):
        remote(k, theirs["o"], full, 2, "p").wait_recv()
        remote(k, theirs["x"], full, 5, "p").wait_recv()
        remote(k, theirs["y"], full, 6, "p").wait_recv()
        remote(k, theirs["d"], lo, 7, "p").wait_recv()
        remote(k, theirs["d"], hi, 8, "p").wait_recv()

    def sent(k):
        for src, rows, chan, to in ((mine["o"], full, 0, "x"), (mine["o"], full, 1, "y"), (mine["o"], full, 2, "p"),
                                    (mine["x"], lo, 3, "y"), (mine["y"], hi, 4, "x"), (mine["x"], full, 5, "p"),
                                    (mine["y"], full, 6, "p"), (mine["d"], lo, 7, "p"), (mine["d"], hi, 8, "p")):
            remote(k, src, rows, chan, to).wait_send()

    def mcopy(o, back=False):
        y2, x2, c2 = flip(o)
        num = c2 * 4 + y2 * 2 + x2
        idx = y2 * 4 + x2 * 2 + c2
        src, dst = (meta.at[num], num) if back else (mout.at[idx], mine["o"])
        return pltpu.make_async_remote_copy(src, meta.at[dst], msend.at[num], mrecv.at[dst],
                                            device_id=dict(ey=y2, ex=x2, ec=c2), device_id_type=MESH)

    for o in others:
        mcopy(o).start()
    direct(0)
    direct(1)

    for hf in range(2):
        acc[0, 0:t, :] = jnp.zeros((t, 2 * f), F32)

        def body(k, _):
            b = hf * NK + k
            fetch(b + NS - 1)
            ready(b)
            acc[0, 0:t, :] += jnp.dot(xg[k, mine["o"]], wb[lax.rem(b, NS)], preferred_element_type=F32)
            return 0

        lax.fori_loop(0, NK, body, 0)
        hst[hf, 0:t, :] = silu_mul(acc[0, 0:t, 0:f], acc[0, 0:t, f:2 * f])
        pltpu.make_async_copy(hst.at[hf, 0:t], sh_ref.at[hf], osem.at[hf]).start()

    relay(0)
    direct(2)

    meta[mine["o"]] = mout[ey * 4 + ex * 2 + ec]
    for o in others:
        mcopy(o, True).wait_recv()
    slots = lax.broadcasted_iota(jnp.int32, (cap, t), 0).astype(F32)

    def build(s, _):
        parts = []
        for e in range(el):
            sel = meta[s, e:e + 1, :] == slots
            disp[s, e * cap:(e + 1) * cap, :] = jnp.where(sel, 1.0, 0.0).astype(BF)
            parts.append(jnp.where(sel, meta[s, el + e:el + e + 1, :], 0.0))
        w = jnp.concatenate(parts, axis=0).T
        n = el * cap
        slot = lax.rem(s, 2)

        @pl.when(s >= 2)
        def _():
            pltpu.make_async_copy(wst.at[slot], wc_ref.at[s - 2], csem.at[slot]).wait()

        for i in range(3):
            p = w.astype(BF)
            wst[slot, :, i * n:(i + 1) * n] = p
            w = w - p.astype(F32)
        pltpu.make_async_copy(wst.at[slot], wc_ref.at[s], csem.at[slot]).start()
        return 0

    lax.fori_loop(0, 8, build, 0)
    relay(1)
    direct(3)

    def gather(k):
        def body(s, _):
            r = jnp.dot(disp[s], xg[k, s], preferred_element_type=F32).astype(BF)
            for e in range(el):
                xe[e, s] = r[e * cap:(e + 1) * cap]
            return 0

        lax.fori_loop(0, 8, body, 0)

    def product(k, e):
        b = nsh + k * el + e
        fetch(b + NS - 1)
        ready(b)
        return jnp.dot(xe[e].reshape(8 * cap, kw), wb[lax.rem(b, NS)], preferred_element_type=F32)

    def start_acc(e, _):
        acc[e] = product(0, e)
        return 0

    corner(0)
    arrived(0)
    gather(0)
    lax.fori_loop(0, el // 2, start_acc, 0)
    relay(2)
    corner(1)
    lax.fori_loop(el // 2, el, start_acc, 0)

    def more(k, _):
        arrived(k)
        gather(k)

        def add(e, _):
            acc[e] += product(k, e)
            return 0

        lax.fori_loop(0, el // 2, add, 0)

        @pl.when(k == 1)
        def _():
            relay(3)
        corner(k + 1)
        lax.fori_loop(el // 2, el, add, 0)
        return 0

    lax.fori_loop(1, NK - 1, more, 0)

    arrived(NK - 1)
    gather(NK - 1)
    for hf in range(2):
        pltpu.make_async_copy(hst.at[hf, 0:t], sh_ref.at[hf], osem.at[hf]).wait()

    def last(e, _):
        slot = lax.rem(e, 2)
        acc[e] += product(NK - 1, e)

        @pl.when(e >= 2)
        def _():
            pltpu.make_async_copy(hst.at[slot], h_ref.at[e - 2], osem.at[slot]).wait()
        hst[slot] = silu_mul(acc[e, :, 0:f], acc[e, :, f:2 * f])
        pltpu.make_async_copy(hst.at[slot], h_ref.at[e], osem.at[slot]).start()
        return 0

    lax.fori_loop(0, el, last, 0)

    for s in (6, 7):
        pltpu.make_async_copy(wst.at[s % 2], wc_ref.at[s], csem.at[s % 2]).wait()
    for e in (el - 2, el - 1):
        pltpu.make_async_copy(hst.at[e % 2], h_ref.at[e], osem.at[e % 2]).wait()
    for o in others:
        mcopy(o).wait_send()
    for k in range(NK):
        sent(k)


def second(el, cap, h_ref, sh_ref, wc_ref, x_ref, w2_ref, ws2_ref, y_ref,
           hv, shv, wcv, xv, wb, o3, part, pr, dr, fr, res, yst,
           hsem, csem, xsem, wsem, ysem, psend, precv, dsend, drecv, fsend, frecv):
    ey, ex, ec, dev, chip = place()
    t, hd = x_ref.shape
    nc = hd // CW
    f = w2_ref.shape[1]
    half = t // 2
    lo, hi = pl.ds(0, half), pl.ds(half, half)
    per = el + 2
    nb = nc * per
    n = el * cap

    def block(b, go):
        c, j = b // per, lax.rem(b, per)
        cols = pl.ds(pl.multiple_of(c * CW, CW), CW)
        slot = lax.rem(b, NW)

        @pl.when((j < el) & (b < nb))
        def _():
            go(pltpu.make_async_copy(w2_ref.at[j, :, cols], wb.at[slot], wsem.at[slot]))

        @pl.when((j >= el) & (b < nb))
        def _():
            rows = pl.ds(pl.multiple_of((j - el) * f, 128), f)
            go(pltpu.make_async_copy(ws2_ref.at[rows, cols], wb.at[slot], wsem.at[slot]))

    def fetch(b):
        block(b, lambda c: c.start())

    def ready(b):
        block(b, lambda c: c.wait())

    def hcopy(e):
        return pltpu.make_async_copy(h_ref.at[e], hv.at[e], hsem.at[e])

    hcopy(0).start()
    for b in range(NW - 1):
        fetch(b)
    for e in range(1, el):
        hcopy(e).start()
    loads = [pltpu.make_async_copy(sh_ref, shv, xsem.at[0]), pltpu.make_async_copy(x_ref, xv, xsem.at[1]),
             pltpu.make_async_copy(wc_ref, wcv, csem)]
    for c in loads:
        c.start()

    barrier = pltpu.get_barrier_semaphore()
    for to in "xyp":
        pl.semaphore_signal(barrier, inc=1, device_id=dev[to], device_id_type=MESH)
    pl.semaphore_wait(barrier, 3)

    def swap(c):
        return pltpu.make_async_remote_copy(part.at[1, c], pr.at[c], psend.at[c], precv.at[c], device_id=dev["p"],
                                            device_id_type=MESH)

    def corner(c, i):
        src = part.at[0, c, chip["d"], (lo, hi)[i]]
        return pltpu.make_async_remote_copy(src, dr.at[c, i], dsend.at[c, i], drecv.at[c, i], device_id=dev["xy"[i]],
                                            device_id_type=MESH)

    def final(c, i, rows):
        src = part.at[0, c, chip["xy"[i]], (lo, hi)[rows]]
        return pltpu.make_async_remote_copy(src, fr.at[c, i, (lo, hi)[rows]], fsend.at[c, i, rows], frecv.at[c, i, rows],
                                            device_id=dev["xy"[i]], device_id_type=MESH)

    def weigh(c, g):
        core = ec if g == 0 else 1 - ec

        def body(ch, _):
            s = core * 4 + ch
            part[g, c, ch] = jnp.dot(wcv[s], o3[s], preferred_element_type=F32)
            return 0

        lax.fori_loop(0, 4, body, 0)

    def compute(c):
        def expert(e, _):
            b = c * per + e
            fetch(b + NW - 1)

            @pl.when(c == 0)
            def _():
                hcopy(e).wait()
            ready(b)
            o = jnp.dot(hv[e], wb[lax.rem(b, NW)], preferred_element_type=F32).astype(BF)
            for s in range(8):
                for i in range(3):
                    o3[s, pl.ds(pl.multiple_of(i * n + e * cap, 16), cap), :] = o[s * cap:(s + 1) * cap]
            return 0

        lax.fori_loop(0, el, expert, 0)

        @pl.when(c == 0)
        def _():
            for d in loads:
                d.wait()
        weigh(c, 1)
        swap(c).start()
        weigh(c, 0)
        s = None
        for i in range(2):
            b = c * per + el + i
            fetch(b + NW - 1)
            ready(b)
            p = jnp.dot(shv[i], wb[lax.rem(b, NW)], preferred_element_type=F32)
            s = p if s is None else s + p
        cols = pl.ds(pl.multiple_of(c * CW, CW), CW)
        res[c] = xv[:, cols].astype(F32) + s.astype(BF).astype(F32)

    def stage1(c):
        swap(c).wait_recv()
        for ch in "dxyo":
            part[0, c, chip[ch]] += pr[c, chip[ch]]
        corner(c, 0).start()
        corner(c, 1).start()
        final(c, 0, 0).start()
        final(c, 1, 1).start()

    def stage2(c):
        corner(c, 0).wait_recv()
        part[0, c, chip["y"], 0:half] += dr[c, 0]
        corner(c, 1).wait_recv()
        part[0, c, chip["x"], half:t] += dr[c, 1]
        final(c, 1, 0).start()
        final(c, 0, 1).start()

    def ycopy(c):
        cols = pl.ds(pl.multiple_of(c * CW, CW), CW)
        return pltpu.make_async_copy(yst.at[lax.rem(c, 2)], y_ref.at[:, cols], ysem.at[lax.rem(c, 2)])

    def stage3(c):
        for i in range(2):
            for rows in range(2):
                final(c, i, rows).wait_recv()

        @pl.when(c >= 2)
        def _():
            ycopy(c - 2).wait()
        yst[lax.rem(c, 2)] = (res[c] + (part[0, c, chip["o"]] + fr[c, 0] + fr[c, 1])).astype(BF)
        ycopy(c).start()

    def step(c, _):
        @pl.when(c < nc)
        def _():
            compute(c)
            stage1(c)

        @pl.when((c >= 1) & (c < nc + 1))
        def _():
            stage2(c - 1)

        @pl.when(c >= 2)
        def _():
            stage3(c - 2)
        return 0

    lax.fori_loop(0, nc + 2, step, 0)
    for c in (nc - 2, nc - 1):
        ycopy(c).wait()

    def drain(c, _):
        swap(c).wait_send()
        for i in range(2):
            corner(c, i).wait_send()
            for rows in range(2):
                final(c, i, rows).wait_send()
        return 0

    lax.fori_loop(0, nc, drain, 0)


def solution(mesh):
    pg = mesh.shape["ey"] * mesh.shape["ex"] * mesh.shape["ec"]

    def local(x, ids, gates, w1, w3, w2, ws1, ws3, ws2):
        t, hd = x.shape
        top = ids.shape[1]
        el, _, f = w1.shape
        ne = el * pg
        cap = min(t, 2 * ((t * top + ne - 1) // ne))
        n = el * cap
        kw = hd // NK
        nc = hd // CW
        idt = jnp.pad(ids.T, ((0, 8 - top), (0, 0)), constant_values=-1)
        gt = jnp.pad(gates.T, ((0, 8 - top), (0, 0)))
        dma = pltpu.SemaphoreType.DMA
        h, sh, wc = pl.pallas_call(
            functools.partial(first, el, cap),
            out_shape=(jax.ShapeDtypeStruct((el, pg * cap, f), BF), jax.ShapeDtypeStruct((2, t, f), BF),
                       jax.ShapeDtypeStruct((pg, t, 3 * n), BF)),
            in_specs=[VM, VM] + [ANY] * 5, out_specs=(ANY,) * 3,
            scratch_shapes=[
                pltpu.VMEM((NK, pg, t, kw), BF), pltpu.VMEM((el, pg * cap, 2 * f), F32), pltpu.VMEM((NS, kw, 2 * f), BF),
                pltpu.VMEM((pg, n, t), BF), pltpu.VMEM((el, pg, cap, kw), BF), pltpu.VMEM((2, pg * cap, f), BF),
                pltpu.VMEM((2, t, 3 * n), BF), pltpu.VMEM((pg, 2 * el, t), F32), pltpu.VMEM((pg, 2 * el, t), F32),
                dma((NK,)), dma((NS, 2)), dma((2,)), dma((2,)), dma((8,)), dma((8,)), dma((NK, 9)), dma((NK, 9))],
            compiler_params=pltpu.CompilerParams(collective_id=0, has_side_effects=True, vmem_limit_bytes=VLIM),
        )(idt, gt, x, w1, w3, ws1, ws3)
        return pl.pallas_call(
            functools.partial(second, el, cap),
            out_shape=jax.ShapeDtypeStruct((t, hd), BF),
            in_specs=[ANY] * 6, out_specs=ANY,
            scratch_shapes=[
                pltpu.VMEM((el, pg * cap, f), BF), pltpu.VMEM((2, t, f), BF), pltpu.VMEM((pg, t, 3 * n), BF),
                pltpu.VMEM((t, hd), BF), pltpu.VMEM((NW, f, CW), BF), pltpu.VMEM((pg, 3 * n, CW), BF),
                pltpu.VMEM((2, nc, 4, t, CW), F32), pltpu.VMEM((nc, 4, t, CW), F32), pltpu.VMEM((nc, 2, t // 2, CW), F32),
                pltpu.VMEM((nc, 2, t, CW), F32), pltpu.VMEM((nc, t, CW), F32), pltpu.VMEM((2, t, CW), BF),
                dma((el,)), dma, dma((2,)), dma((NW,)), dma((2,)), dma((nc,)), dma((nc,)), dma((nc, 2)), dma((nc, 2)),
                dma((nc, 2, 2)), dma((nc, 2, 2))],
            compiler_params=pltpu.CompilerParams(collective_id=1, has_side_effects=True, vmem_limit_bytes=VLIM),
        )(h, sh, wc, x, w2, ws2)

    return jax.shard_map(local, mesh=mesh,
                         in_specs=(P(ALL), P(ALL), P(ALL), P(EXP), P(EXP), P(EXP), P(), P(), P()),
                         out_specs=P(ALL), check_vma=False)
```

time: 448 us -> 184 us (0.41)
  Pallas kernels: 0 us -> 179 us
  blocking collectives: 143 us -> 0 us
  waiting for transfers between devices: 129 us -> 0 us
  matrix products: 112 us -> 0 us
  local copies, waits for them, and re-layouts: 46.9 us -> 4.9 us
  other arithmetic: 11.8 us -> 0 us
    pallas_call x0 -> x2, Pallas kernels: none -> 179 us  [the longest x1 92.2 us: local(): pl.pallas_call(functools.partial(second, el, cap), out_shape=jax.ShapeDty...]
    all_to_all x1 -> x0, blocking collectives: 143 us -> none  [local(): recv = lax.all_to_all(send, EXP, 0, 0, tiled=True)]
    all_to_all x1 -> x0, waiting for transfers between devices: 129 us -> none  [local(): back = lax.all_to_all(out, EXP, 0, 0, tiled=True)]
    dot_general x6 -> x0, matrix products: 112 us -> none  [the longest x1 50.3 us: local(): jnp.einsum('erf,efh->erh', hid, w2, preferred_element_type=jnp.float32)]
    gather x1 -> x0, local copies, waits for them, and re-layouts: 18.9 us -> none  [local(): got = back[pos].reshape(t, top, hd)]
    reshape x3 -> x0, local copies, waits for them, and re-layouts: 15.9 us -> none  [the longest x1 10.7 us: local(): out.reshape(el, pg, cap, hd).transpose(1, 0, 2, 3)]
    convert_element_type x1 -> x0, local copies, waits for them, and re-layouts: 11.7 us -> none  [local(): moe = jnp.sum(gates[:, :, None] * got.astype(jnp.float32), axis=1)]
    reduce_sum x2 -> x0, other arithmetic: 9.53 us -> none  [the longest x1 9.48 us: local(): moe = jnp.sum(gates[:, :, None] * got.astype(jnp.float32), axis=1)]
  transfers between devices with their start and end apart: 1 -> 0, of which waited for: 1 -> 0; matrix products, arithmetic and copies ran while one was open for 2% -> 0% of each run, Pallas kernels for 0% -> 0%
where the time goes in v2:
time: 184 us
  Pallas kernels  179 us (97%)
  local copies, waits for them, and re-layouts  4.9 us (3%)
    pallas_call x1, Pallas kernels, local(): pl.pallas_call(functools.partial(second, el, cap), out_shape=jax.ShapeDty...  92.2 us
    pallas_call x1, Pallas kernels, local(): pl.pallas_call(functools.partial(first, el, cap), out_shape=(jax.ShapeDty...  86.9 us

profile of v2, /device:TPU:0, one launch (start us, length us, event | category | flops | bytes accessed | tf_op | source)
XLA Modules:
  0.0 184.0 jit_solution(11485697233021865275)
XLA Ops:
  0.0 1.3 pad.8.ids_ref
  1.3 1.3 pad.9.gates_ref
  2.6 86.9 %shard_map.91 = (bf16[8,384,1408]{2,1,0:T(8,128)(2,1)}, bf16[2,256,1408]{2,1,0:T(8,128)(2,1)}, bf16[8,256,1152]{2,1,0:T(8,128)(2,1)}) custom-call(s32[8,256]{1,0:T(8,128)} %pad.8.ids_ref, f32[8,256]{1,0:T(8,128)} %pad.9.gates_ref, bf16[256,2048]{1,0:T(8,128)(2,1)} %x_ref.3, bf16[8,2048,1408]{2,1,0:T(8,128)(2,1)} %w1_ref.1, bf16[8,2048,1408]{2,1,0:T(8,128)(2,1)} %w3_ref.1, ...), custom_call_target="tpu_custom_call" | custom-call | tf_op jit(solution)/shard_map/pallas_call | solution.py:463
  89.5 92.2 %shard_map.92 = bf16[256,2048]{1,0:T(8,128)(2,1)} custom-call(bf16[8,384,1408]{2,1,0:T(8,128)(2,1)} %get-tuple-element.8.h_ref, bf16[2,256,1408]{2,1,0:T(8,128)(2,1)} %get-tuple-element.9.sh_ref, bf16[8,256,1152]{2,1,0:T(8,128)(2,1)} %get-tuple-element.10.wc_ref, bf16[256,2048]{1,0:T(8,128)(2,1)} %x_ref.3, bf16[8,1408,2048]{2,1,0:T(8,128)(2,1)} %w2_ref.1, ...), custom_call_target="tpu_custom_call" | custom-call | tf_op jit(solution)/shard_map/pallas_call | solution.py:475
  181.7 2.3 %copy.11 = bf16[256,2048]{1,0:T(8,128)(2,1)} copy(bf16[256,2048]{1,0:T(8,128)(2,1)} %shard_map.92) | data formatting | bytes 2097152

commit v3 on v2

--- a/solution.py
+++ b/solution.py
@@ -20,6 +20,7 @@
 NS = 3
 CW = 256
 NW = 4
+LAG = 3
 
 
 def place():
@@ -33,59 +34,62 @@
     return (a * jax.nn.sigmoid(a) * b).astype(BF)
 
 
-def first(el, cap, ids_ref, gates_ref, x_ref, w1_ref, w3_ref, ws1_ref, ws3_ref, h_ref, sh_ref, wc_ref,
-          xg, acc, wb, disp, xe, hst, wst, mout, meta,
-          xsem, wsem, osem, csem, msend, mrecv, ssem, rsem):
+def first(el, cap, ids_ref, gates_ref, x_ref, ws1_ref, ws3_ref, ws2_ref, xe_ref, res_ref, wc_ref, cnt_ref,
+          xg, acc, sh, wb, wd, disp, xst, rst, wst, cst, mout, meta,
+          xsem, wsem, dsem, gsem, osem, csem, nsem, msend, mrecv, ssem, rsem):
     ey, ex, ec, dev, chip = place()
-    t = x_ref.shape[0]
-    kw = x_ref.shape[1] // NK
-    f = w1_ref.shape[2]
+    t, hd = x_ref.shape
+    top = ids_ref.shape[1]
+    kw = hd // NK
+    f = ws1_ref.shape[1] // 2
+    nc = hd // CW
     half = t // 2
+    n = el * cap
     lo, hi, full = pl.ds(0, half), pl.ds(half, half), pl.ds(0, t)
     mine = {c: ec * 4 + chip[c] for c in "oxyd"}
     theirs = {c: (1 - ec) * 4 + chip[c] for c in "oxyd"}
-    nsh = 2 * NK
-    nb = nsh + NK * el
+    nb = 2 * NK
 
     def block(b, go):
-        slot = lax.rem(b, NS)
-
-        @pl.when(b < nsh)
-        def _():
+        @pl.when(b < nb)
+        def _():
+            slot = lax.rem(b, NS)
             rows = pl.ds(pl.multiple_of(lax.rem(b, NK) * kw, kw), kw)
             cols = pl.ds(pl.multiple_of((b // NK) * f, 128), f)
             for i, w in enumerate((ws1_ref, ws3_ref)):
                 go(pltpu.make_async_copy(w.at[rows, cols], wb.at[slot, :, pl.ds(i * f, f)], wsem.at[slot, i]))
 
-        @pl.when((b >= nsh) & (b < nb))
-        def _():
-            q = b - nsh
-            rows = pl.ds(pl.multiple_of((q // el) * kw, kw), kw)
-            for i, w in enumerate((w1_ref, w3_ref)):
-                go(pltpu.make_async_copy(w.at[lax.rem(q, el), rows], wb.at[slot, :, pl.ds(i * f, f)], wsem.at[slot, i]))
-
-    def fetch(b):
-        block(b, lambda c: c.start())
-
-    def ready(b):
-        block(b, lambda c: c.wait())
-
-    for b in range(NS - 1):
-        fetch(b)
+    def down(c, go):
+        @pl.when(c < nc)
+        def _():
+            slot = lax.rem(c, NS)
+            cols = pl.ds(pl.multiple_of(c * CW, CW), CW)
+            go(pltpu.make_async_copy(ws2_ref.at[:, cols], wd.at[slot], dsem.at[slot]))
+
+    def go_start(c):
+        c.start()
+
+    def go_wait(c):
+        c.wait()
+
     for k in range(NK):
         pltpu.make_async_copy(x_ref.at[:, pl.ds(k * kw, kw)], xg.at[k, mine["o"]], xsem.at[k]).start()
-
-    ne = el * 8
-    row = lax.broadcasted_iota(jnp.int32, (ne, t), 0)
-    chosen = jnp.zeros((ne, t), F32)
-    gate = jnp.zeros((ne, t), F32)
-    for j in range(6):
-        hit = ids_ref[j:j + 1, :] == row
+    for b in range(NS - 1):
+        block(b, go_start)
+    for c in range(NS - 1):
+        down(c, go_start)
+
+    col = lax.broadcasted_iota(jnp.int32, (t, 128), 1)
+    chosen = jnp.zeros((t, 128), F32)
+    gate = jnp.zeros((t, 128), F32)
+    for j in range(top):
+        hit = ids_ref[:, j:j + 1] == col
         chosen = jnp.where(hit, 1.0, chosen)
-        gate = jnp.where(hit, gates_ref[j:j + 1, :], gate)
-    before = (lax.broadcasted_iota(jnp.int32, (t, t), 0) < lax.broadcasted_iota(jnp.int32, (t, t), 1))
-    rank = jnp.dot(chosen.astype(BF), before.astype(F32).astype(BF), preferred_element_type=F32)
-    rank = jnp.where(chosen > 0.0, rank, -1.0)
+        gate = jnp.where(hit, gates_ref[:, j:j + 1], gate)
+    before = lax.broadcasted_iota(jnp.int32, (t, t), 1) < lax.broadcasted_iota(jnp.int32, (t, t), 0)
+    rank = jnp.dot(jnp.where(before, 1.0, 0.0).astype(BF), chosen.astype(BF), preferred_element_type=F32)
+    rank = jnp.where(chosen > 0.0, rank, -1.0).T
+    gate = gate.T
     for d in range(8):
         mout[d, 0:el, :] = rank[d * el:(d + 1) * el]
         mout[d, el:2 * el, :] = gate[d * el:(d + 1) * el]
@@ -101,15 +105,13 @@
         pl.semaphore_signal(barrier, inc=1, device_id=dict(ey=y2, ex=x2, ec=c2), device_id_type=MESH)
     pl.semaphore_wait(barrier, len(others))
 
-    for k in range(NK):
-        pltpu.make_async_copy(x_ref.at[:, pl.ds(k * kw, kw)], xg.at[k, mine["o"]], xsem.at[k]).wait()
-
     def remote(k, src, rows, chan, to):
         ref = xg.at[k, src, rows]
         return pltpu.make_async_remote_copy(ref, ref, ssem.at[k, chan], rsem.at[k, chan], device_id=dev[to],
                                             device_id_type=MESH)
 
     def direct(k):
+        pltpu.make_async_copy(x_ref.at[:, pl.ds(k * kw, kw)], xg.at[k, mine["o"]], xsem.at[k]).wait()
         for chan, to in enumerate("xyp"):
             remote(k, mine["o"], full, chan, to).start()
 
@@ -148,27 +150,31 @@
         return pltpu.make_async_remote_copy(src, meta.at[dst], msend.at[num], mrecv.at[dst],
                                             device_id=dict(ey=y2, ex=x2, ec=c2), device_id_type=MESH)
 
+    direct(0)
     for o in others:
         mcopy(o).start()
-    direct(0)
     direct(1)
+    for k in range(2, NK):
+        pltpu.make_async_copy(x_ref.at[:, pl.ds(k * kw, kw)], xg.at[k, mine["o"]], xsem.at[k]).wait()
 
     for hf in range(2):
-        acc[0, 0:t, :] = jnp.zeros((t, 2 * f), F32)
+        acc[...] = jnp.zeros((t, 2 * f), F32)
 
         def body(k, _):
             b = hf * NK + k
-            fetch(b + NS - 1)
-            ready(b)
-            acc[0, 0:t, :] += jnp.dot(xg[k, mine["o"]], wb[lax.rem(b, NS)], preferred_element_type=F32)
+            block(b + NS - 1, go_start)
+            block(b, go_wait)
+            acc[...] += jnp.dot(xg[k, mine["o"]], wb[lax.rem(b, NS)], preferred_element_type=F32)
             return 0
 
         lax.fori_loop(0, NK, body, 0)
-        hst[hf, 0:t, :] = silu_mul(acc[0, 0:t, 0:f], acc[0, 0:t, f:2 * f])
-        pltpu.make_async_copy(hst.at[hf, 0:t], sh_ref.at[hf], osem.at[hf]).start()
+        sh[:, hf * f:(hf + 1) * f] = silu_mul(acc[:, 0:f], acc[:, f:2 * f])
 
     relay(0)
-    direct(2)
+    for k in range(2, NK):
+        for chan, to in enumerate("xyp"):
+            if k == 2:
+                remote(k, mine["o"], full, chan, to).start()
 
     meta[mine["o"]] = mout[ey * 4 + ex * 2 + ec]
     for o in others:
@@ -182,8 +188,9 @@
             disp[s, e * cap:(e + 1) * cap, :] = jnp.where(sel, 1.0, 0.0).astype(BF)
             parts.append(jnp.where(sel, meta[s, el + e:el + e + 1, :], 0.0))
         w = jnp.concatenate(parts, axis=0).T
-        n = el * cap
         slot = lax.rem(s, 2)
+        most = jnp.max(meta[s, 0:el, :], axis=1, keepdims=True).astype(jnp.int32) + 1
+        cst[pl.ds(pl.multiple_of(s * el, 8), el), :] = jnp.broadcast_to(most, (el, 128))
 
         @pl.when(s >= 2)
         def _():
@@ -197,93 +204,184 @@
         return 0
 
     lax.fori_loop(0, 8, build, 0)
+    counts = pltpu.make_async_copy(cst, cnt_ref, nsem)
+    counts.start()
+
+    def rcopy(c):
+        return pltpu.make_async_copy(rst.at[lax.rem(c, 2)], res_ref.at[c], osem.at[lax.rem(c, 2)])
+
+    def shared_down(c, _):
+        down(c + NS - 1, go_start)
+        down(c, go_wait)
+
+        @pl.when(c >= 2)
+        def _():
+            rcopy(c - 2).wait()
+        v = jnp.dot(sh[...], wd[lax.rem(c, NS)], preferred_element_type=F32).astype(BF).astype(F32)
+        per = kw // CW
+        cols = pl.ds(pl.multiple_of(lax.rem(c, per) * CW, CW), CW)
+        rst[lax.rem(c, 2)] = xg[c // per, mine["o"], :, cols].astype(F32) + v
+        rcopy(c).start()
+        return 0
+
+    lax.fori_loop(0, nc // 2, shared_down, 0)
     relay(1)
-    direct(3)
+    for chan, to in enumerate("xyp"):
+        remote(3, mine["o"], full, chan, to).start()
+    lax.fori_loop(nc // 2, nc, shared_down, 0)
+
+    def gcopy(k, s):
+        slot = lax.rem(s, 2)
+        return pltpu.make_async_copy(xst.at[slot], xe_ref.at[:, s, :, pl.ds(pl.multiple_of(k * kw, kw), kw)], gsem.at[slot])
 
     def gather(k):
         def body(s, _):
             r = jnp.dot(disp[s], xg[k, s], preferred_element_type=F32).astype(BF)
+            if isinstance(k, int) and k == 0:
+                @pl.when(s >= 2)
+                def _():
+                    gcopy(k, s - 2).wait()
+            else:
+                @pl.when(s < 2)
+                def _():
+                    gcopy(k - 1, s + 6).wait()
+
+                @pl.when(s >= 2)
+                def _():
+                    gcopy(k, s - 2).wait()
             for e in range(el):
-                xe[e, s] = r[e * cap:(e + 1) * cap]
+                xst[lax.rem(s, 2), e] = r[e * cap:(e + 1) * cap]
+            gcopy(k, s).start()
             return 0
 
         lax.fori_loop(0, 8, body, 0)
-
-    def product(k, e):
-        b = nsh + k * el + e
-        fetch(b + NS - 1)
-        ready(b)
-        return jnp.dot(xe[e].reshape(8 * cap, kw), wb[lax.rem(b, NS)], preferred_element_type=F32)
-
-    def start_acc(e, _):
-        acc[e] = product(0, e)
-        return 0
 
     corner(0)
     arrived(0)
     gather(0)
-    lax.fori_loop(0, el // 2, start_acc, 0)
     relay(2)
     corner(1)
-    lax.fori_loop(el // 2, el, start_acc, 0)
-
-    def more(k, _):
-        arrived(k)
-        gather(k)
-
-        def add(e, _):
-            acc[e] += product(k, e)
-            return 0
-
-        lax.fori_loop(0, el // 2, add, 0)
-
-        @pl.when(k == 1)
-        def _():
-            relay(3)
-        corner(k + 1)
-        lax.fori_loop(el // 2, el, add, 0)
-        return 0
-
-    lax.fori_loop(1, NK - 1, more, 0)
-
-    arrived(NK - 1)
-    gather(NK - 1)
-    for hf in range(2):
-        pltpu.make_async_copy(hst.at[hf, 0:t], sh_ref.at[hf], osem.at[hf]).wait()
-
-    def last(e, _):
-        slot = lax.rem(e, 2)
-        acc[e] += product(NK - 1, e)
-
-        @pl.when(e >= 2)
-        def _():
-            pltpu.make_async_copy(hst.at[slot], h_ref.at[e - 2], osem.at[slot]).wait()
-        hst[slot] = silu_mul(acc[e, :, 0:f], acc[e, :, f:2 * f])
-        pltpu.make_async_copy(hst.at[slot], h_ref.at[e], osem.at[slot]).start()
-        return 0
-
-    lax.fori_loop(0, el, last, 0)
+    arrived(1)
+    gather(1)
+    relay(3)
+    corner(2)
+    arrived(2)
+    gather(2)
+    corner(3)
+    arrived(3)
+    gather(3)
 
     for s in (6, 7):
+        gcopy(NK - 1, s).wait()
         pltpu.make_async_copy(wst.at[s % 2], wc_ref.at[s], csem.at[s % 2]).wait()
-    for e in (el - 2, el - 1):
-        pltpu.make_async_copy(hst.at[e % 2], h_ref.at[e], osem.at[e % 2]).wait()
+    for c in (nc - 2, nc - 1):
+        rcopy(c).wait()
+    counts.wait()
     for o in others:
         mcopy(o).wait_send()
-    for k in range(NK):
+
+    def drain(k, _):
         sent(k)
-
-
-def second(el, cap, h_ref, sh_ref, wc_ref, x_ref, w2_ref, ws2_ref, y_ref,
-           hv, shv, wcv, xv, wb, o3, part, pr, dr, fr, res, yst,
+        return 0
+
+    lax.fori_loop(0, NK, drain, 0)
+
+
+def middle(el, cap, cnt_ref, xe_ref, w1_ref, w3_ref, h_ref, xc, wb, hs, zero, wsem, xsem, osem):
+    f = w1_ref.shape[2]
+    hd = w1_ref.shape[1]
+    pc = 16
+    rows = 8 * cap
+
+    def pieces(e, go, skip=None):
+        off = 0
+        for s in range(8):
+            n = cnt_ref[s * el + e, 0]
+            for r in range(cap // pc):
+                at = pl.ds(r * pc, pc)
+                if skip is None:
+                    pl.when(n > r * pc)(functools.partial(go, s, at, off + r * pc))
+                else:
+                    pl.when(n > r * pc)(functools.partial(go, s, at, off + r * pc))
+                    pl.when(n <= r * pc)(functools.partial(skip, s, at))
+            off += (n + pc - 1) // pc * pc
+        return off
+
+    def rows_in(e, op):
+        slot = lax.rem(e, 2)
+
+        def go(s, at, off):
+            op(pltpu.make_async_copy(xe_ref.at[e, s, at], xc.at[slot, pl.ds(pl.multiple_of(off, pc), pc)], xsem.at[slot]))
+        return pieces(e, go)
+
+    def rows_out(e, op):
+        slot = lax.rem(e, 2)
+
+        def go(s, at, off):
+            op(pltpu.make_async_copy(hs.at[slot, pl.ds(pl.multiple_of(off, pc), pc)], h_ref.at[e, s, at], osem.at[slot]))
+
+        def skip(s, at):
+            op(pltpu.make_async_copy(zero, h_ref.at[e, s, at], osem.at[slot]))
+        pieces(e, go, skip)
+
+    def weights(e, op):
+        slot = lax.rem(e, 2)
+        q = hd // 2
+        for i, w in enumerate((w1_ref, w3_ref)):
+            for j in range(2):
+                at = pl.ds(j * q, q)
+                op(pltpu.make_async_copy(w.at[e, at], wb.at[slot, at, pl.ds(i * f, f)], wsem.at[slot]))
+
+    def start(c):
+        c.start()
+
+    def wait(c):
+        c.wait()
+
+    rows_in(0, start)
+    weights(0, start)
+    rows_in(1, start)
+    weights(1, start)
+    zero[...] = jnp.zeros_like(zero)
+
+    def body(e, _):
+        slot = lax.rem(e, 2)
+        total = rows_in(e, wait)
+        weights(e, wait)
+
+        @pl.when(e >= 2)
+        def _():
+            rows_out(e - 2, wait)
+
+        def go(m):
+            d = jnp.dot(xc[slot, 0:m], wb[slot], preferred_element_type=F32)
+            hs[slot, 0:m] = silu_mul(d[:, 0:f], d[:, f:2 * f])
+
+        step = rows // 3
+        for i in range(1, 4):
+            pl.when((total <= i * step) & (total > (i - 1) * step))(functools.partial(go, i * step))
+        rows_out(e, start)
+
+        @pl.when(e + 2 < el)
+        def _():
+            rows_in(e + 2, start)
+            weights(e + 2, start)
+        return 0
+
+    lax.fori_loop(0, el, body, 0)
+    rows_out(el - 2, wait)
+    rows_out(el - 1, wait)
+
+
+def second(el, cap, h_ref, wc_ref, res_ref, w2_ref, y_ref,
+           hv, wcv, wb, o3, part, pr, dr, fr, res, yst,
            hsem, csem, xsem, wsem, ysem, psend, precv, dsend, drecv, fsend, frecv):
     ey, ex, ec, dev, chip = place()
-    t, hd = x_ref.shape
+    t, hd = y_ref.shape
     nc = hd // CW
-    f = w2_ref.shape[1]
     half = t // 2
     lo, hi = pl.ds(0, half), pl.ds(half, half)
-    per = el + 2
+    per = el
     nb = nc * per
     n = el * cap
 
@@ -292,14 +390,9 @@
         cols = pl.ds(pl.multiple_of(c * CW, CW), CW)
         slot = lax.rem(b, NW)
 
-        @pl.when((j < el) & (b < nb))
+        @pl.when(b < nb)
         def _():
             go(pltpu.make_async_copy(w2_ref.at[j, :, cols], wb.at[slot], wsem.at[slot]))
-
-        @pl.when((j >= el) & (b < nb))
-        def _():
-            rows = pl.ds(pl.multiple_of((j - el) * f, 128), f)
-            go(pltpu.make_async_copy(ws2_ref.at[rows, cols], wb.at[slot], wsem.at[slot]))
 
     def fetch(b):
         block(b, lambda c: c.start())
@@ -315,8 +408,7 @@
         fetch(b)
     for e in range(1, el):
         hcopy(e).start()
-    loads = [pltpu.make_async_copy(sh_ref, shv, xsem.at[0]), pltpu.make_async_copy(x_ref, xv, xsem.at[1]),
-             pltpu.make_async_copy(wc_ref, wcv, csem)]
+    loads = [pltpu.make_async_copy(wc_ref, wcv, csem), pltpu.make_async_copy(res_ref, res, xsem)]
     for c in loads:
         c.start()
 
@@ -373,15 +465,6 @@
         weigh(c, 1)
         swap(c).start()
         weigh(c, 0)
-        s = None
-        for i in range(2):
-            b = c * per + el + i
-            fetch(b + NW - 1)
-            ready(b)
-            p = jnp.dot(shv[i], wb[lax.rem(b, NW)], preferred_element_type=F32)
-            s = p if s is None else s + p
-        cols = pl.ds(pl.multiple_of(c * CW, CW), CW)
-        res[c] = xv[:, cols].astype(F32) + s.astype(BF).astype(F32)
 
     def stage1(c):
         swap(c).wait_recv()
@@ -425,12 +508,12 @@
         def _():
             stage2(c - 1)
 
-        @pl.when(c >= 2)
-        def _():
-            stage3(c - 2)
+        @pl.when(c >= LAG)
+        def _():
+            stage3(c - LAG)
         return 0
 
-    lax.fori_loop(0, nc + 2, step, 0)
+    lax.fori_loop(0, nc + LAG, step, 0)
     for c in (nc - 2, nc - 1):
         ycopy(c).wait()
 
@@ -457,34 +540,43 @@
         n = el * cap
         kw = hd // NK
         nc = hd // CW
-        idt = jnp.pad(ids.T, ((0, 8 - top), (0, 0)), constant_values=-1)
-        gt = jnp.pad(gates.T, ((0, 8 - top), (0, 0)))
         dma = pltpu.SemaphoreType.DMA
-        h, sh, wc = pl.pallas_call(
+        xe, res, wc, cnt = pl.pallas_call(
             functools.partial(first, el, cap),
-            out_shape=(jax.ShapeDtypeStruct((el, pg * cap, f), BF), jax.ShapeDtypeStruct((2, t, f), BF),
-                       jax.ShapeDtypeStruct((pg, t, 3 * n), BF)),
-            in_specs=[VM, VM] + [ANY] * 5, out_specs=(ANY,) * 3,
+            out_shape=(jax.ShapeDtypeStruct((el, pg, cap, hd), BF), jax.ShapeDtypeStruct((nc, t, CW), F32),
+                       jax.ShapeDtypeStruct((pg, t, 3 * n), BF), jax.ShapeDtypeStruct((pg * el, 128), jnp.int32)),
+            in_specs=[VM, VM] + [ANY] * 4, out_specs=(ANY,) * 4,
             scratch_shapes=[
-                pltpu.VMEM((NK, pg, t, kw), BF), pltpu.VMEM((el, pg * cap, 2 * f), F32), pltpu.VMEM((NS, kw, 2 * f), BF),
-                pltpu.VMEM((pg, n, t), BF), pltpu.VMEM((el, pg, cap, kw), BF), pltpu.VMEM((2, pg * cap, f), BF),
-                pltpu.VMEM((2, t, 3 * n), BF), pltpu.VMEM((pg, 2 * el, t), F32), pltpu.VMEM((pg, 2 * el, t), F32),
-                dma((NK,)), dma((NS, 2)), dma((2,)), dma((2,)), dma((8,)), dma((8,)), dma((NK, 9)), dma((NK, 9))],
+                pltpu.VMEM((NK, pg, t, kw), BF), pltpu.VMEM((t, 2 * f), F32), pltpu.VMEM((t, 2 * f), BF),
+                pltpu.VMEM((NS, kw, 2 * f), BF), pltpu.VMEM((NS, 2 * f, CW), BF), pltpu.VMEM((pg, n, t), BF),
+                pltpu.VMEM((2, el, cap, kw), BF), pltpu.VMEM((2, t, CW), F32), pltpu.VMEM((2, t, 3 * n), BF),
+                pltpu.VMEM((pg * el, 128), jnp.int32), pltpu.VMEM((pg, 2 * el, t), F32), pltpu.VMEM((pg, 2 * el, t), F32),
+                dma((NK,)), dma((NS, 2)), dma((NS,)), dma((2,)), dma((2,)), dma((2,)), dma, dma((8,)), dma((8,)),
+                dma((NK, 9)), dma((NK, 9))],
             compiler_params=pltpu.CompilerParams(collective_id=0, has_side_effects=True, vmem_limit_bytes=VLIM),
-        )(idt, gt, x, w1, w3, ws1, ws3)
+        )(ids, gates, x, ws1, ws3, ws2)
+        h = pl.pallas_call(
+            functools.partial(middle, el, cap),
+            out_shape=jax.ShapeDtypeStruct((el, pg, cap, f), BF),
+            in_specs=[pl.BlockSpec(memory_space=pltpu.SMEM)] + [ANY] * 3, out_specs=ANY,
+            scratch_shapes=[
+                pltpu.VMEM((2, pg * cap, hd), BF), pltpu.VMEM((2, hd, 2 * f), BF), pltpu.VMEM((2, pg * cap, f), BF),
+                pltpu.VMEM((16, f), BF), dma((2,)), dma((2,)), dma((2,))],
+            compiler_params=pltpu.CompilerParams(vmem_limit_bytes=VLIM),
+        )(cnt, xe, w1, w3)
         return pl.pallas_call(
             functools.partial(second, el, cap),
             out_shape=jax.ShapeDtypeStruct((t, hd), BF),
-            in_specs=[ANY] * 6, out_specs=ANY,
+            in_specs=[ANY] * 4, out_specs=ANY,
             scratch_shapes=[
-                pltpu.VMEM((el, pg * cap, f), BF), pltpu.VMEM((2, t, f), BF), pltpu.VMEM((pg, t, 3 * n), BF),
-                pltpu.VMEM((t, hd), BF), pltpu.VMEM((NW, f, CW), BF), pltpu.VMEM((pg, 3 * n, CW), BF),
+                pltpu.VMEM((el, pg * cap, f), BF), pltpu.VMEM((pg, t, 3 * n), BF),
+                pltpu.VMEM((NW, f, CW), BF), pltpu.VMEM((pg, 3 * n, CW), BF),
                 pltpu.VMEM((2, nc, 4, t, CW), F32), pltpu.VMEM((nc, 4, t, CW), F32), pltpu.VMEM((nc, 2, t // 2, CW), F32),
                 pltpu.VMEM((nc, 2, t, CW), F32), pltpu.VMEM((nc, t, CW), F32), pltpu.VMEM((2, t, CW), BF),
-                dma((el,)), dma, dma((2,)), dma((NW,)), dma((2,)), dma((nc,)), dma((nc,)), dma((nc, 2)), dma((nc, 2)),
+                dma((el,)), dma, dma, dma((NW,)), dma((2,)), dma((nc,)), dma((nc,)), dma((nc, 2)), dma((nc, 2)),
                 dma((nc, 2, 2)), dma((nc, 2, 2))],
             compiler_params=pltpu.CompilerParams(collective_id=1, has_side_effects=True, vmem_limit_bytes=VLIM),
-        )(h, sh, wc, x, w2, ws2)
+        )(h.reshape(el, pg * cap, f), wc, res, w2)
 
     return jax.shard_map(local, mesh=mesh,
                          in_specs=(P(ALL), P(ALL), P(ALL), P(EXP), P(EXP), P(EXP), P(), P(), P()),

time: 184 us -> 184 us (level)
    pallas_call x0 -> x1, Pallas kernels: none -> 40 us  [local(): pl.pallas_call(functools.partial(middle, el, cap), out_shape=jax.ShapeDty...]
    pallas_call x1, Pallas kernels: 86.9 us -> 51.1 us  [local(): pl.pallas_call(functools.partial(first, el, cap), out_shape=(jax.ShapeDty...]
    pallas_call x1, Pallas kernels: 92.2 us -> 86.8 us  [local(): pl.pallas_call(functools.partial(second, el, cap), out_shape=jax.ShapeDty...]
    unnamed x1 -> x3, local copies, waits for them, and re-layouts: 2.3 us -> 5.3 us
    pad x2 -> x0, local copies, waits for them, and re-layouts: 2.59 us -> none  [the longest x1 1.3 us: local(): idt = jnp.pad(ids.T, ((0, 8 - top), (0, 0)), constant_values=-1)]
where the time goes in v3:
time: 184 us; the launch traced here: 183 us
  Pallas kernels  178 us (97%)
  local copies, waits for them, and re-layouts  5.3 us (3%)
    pallas_call x1, Pallas kernels, local(): pl.pallas_call(functools.partial(second, el, cap), out_shape=jax.ShapeDty...  86.8 us
    pallas_call x1, Pallas kernels, local(): pl.pallas_call(functools.partial(first, el, cap), out_shape=(jax.ShapeDty...  51.1 us
    pallas_call x1, Pallas kernels, local(): pl.pallas_call(functools.partial(middle, el, cap), out_shape=jax.ShapeDty...  40 us
    unnamed x3, local copies, waits for them, and re-layouts  5.3 us

profile of v3, /device:TPU:0, one launch (start us, length us, event | category | flops | bytes accessed | tf_op | source)
XLA Modules:
  0.0 183.2 jit_solution(1797202684523426143)
XLA Ops:
  0.0 1.5 copy.10.ids_ref
  1.5 1.5 copy.11.gates_ref
  3.0 51.1 %shard_map.91 = (bf16[8,8,48,2048]{3,2,1,0:T(8,128)(2,1)}, f32[8,256,256]{2,1,0:T(8,128)}, bf16[8,256,1152]{2,1,0:T(8,128)(2,1)}, s32[64,128]{1,0:T(8,128)}) custom-call(s32[256,6]{1,0:T(8,128)} %copy.10.ids_ref, f32[256,6]{1,0:T(8,128)} %copy.11.gates_ref, bf16[256,2048]{1,0:T(8,128)(2,1)} %x_ref.1, bf16[2048,2816]{1,0:T(8,128)(2,1)} %ws1_ref.1, ...), custom_call_target="tpu_custom_call" | custom-call | tf_op jit(solution)/shard_map/pallas_call | solution.py:544
  54.1 40.0 %shard_map.92 = bf16[8,8,48,1408]{3,2,1,0:T(8,128)(2,1)} custom-call(s32[64,128]{1,0:T(8,128)} %get-tuple-element.9.cnt_ref, bf16[8,8,48,2048]{3,2,1,0:T(8,128)(2,1)} %get-tuple-element.10.xe_ref, bf16[8,2048,1408]{2,1,0:T(8,128)(2,1)} %w1_ref.1, bf16[8,2048,1408]{2,1,0:T(8,128)(2,1)} %w3_ref.1), custom_call_target="tpu_custom_call" | custom-call | tf_op jit(solution)/shard_map/pallas_call | solution.py:558
  94.1 86.8 %shard_map.93 = bf16[256,2048]{1,0:T(8,128)(2,1)} custom-call(bf16[8,384,1408]{2,1,0:T(8,128)(2,1)} %bitcast.1, bf16[8,256,1152]{2,1,0:T(8,128)(2,1)} %get-tuple-element.11.wc_ref, f32[8,256,256]{2,1,0:T(8,128)} %get-tuple-element.12.res_ref, bf16[8,1408,2048]{2,1,0:T(8,128)(2,1)} %w2_ref.1), custom_call_target="tpu_custom_call" | custom-call | tf_op jit(solution)/shard_map/pallas_call | solution.py:567
  180.9 2.3 %copy.13 = bf16[256,2048]{1,0:T(8,128)(2,1)} copy(bf16[256,2048]{1,0:T(8,128)(2,1)} %shard_map.93) | data formatting | bytes 2097152

commit v4 on v2

--- a/solution.py
+++ b/solution.py
@@ -20,6 +20,8 @@
 NS = 3
 CW = 256
 NW = 4
+LAG = 3
+SLAB = 256
 
 
 def place():
@@ -33,8 +35,8 @@
     return (a * jax.nn.sigmoid(a) * b).astype(BF)
 
 
-def first(el, cap, ids_ref, gates_ref, x_ref, w1_ref, w3_ref, ws1_ref, ws3_ref, h_ref, sh_ref, wc_ref,
-          xg, acc, wb, disp, xe, hst, wst, mout, meta,
+def first(el, cap, ids_ref, gates_ref, x_ref, w1_ref, w3_ref, ws1_ref, ws3_ref, h_ref, sh_ref, meta_ref,
+          xg, acc, wb, disp, xe, hst, mout, meta,
           xsem, wsem, osem, csem, msend, mrecv, ssem, rsem):
     ey, ex, ec, dev, chip = place()
     t = x_ref.shape[0]
@@ -79,7 +81,7 @@
     row = lax.broadcasted_iota(jnp.int32, (ne, t), 0)
     chosen = jnp.zeros((ne, t), F32)
     gate = jnp.zeros((ne, t), F32)
-    for j in range(6):
+    for j in range(ids_ref.shape[0]):
         hit = ids_ref[j:j + 1, :] == row
         chosen = jnp.where(hit, 1.0, chosen)
         gate = jnp.where(hit, gates_ref[j:j + 1, :], gate)
@@ -173,27 +175,14 @@
     meta[mine["o"]] = mout[ey * 4 + ex * 2 + ec]
     for o in others:
         mcopy(o, True).wait_recv()
+    keep = pltpu.make_async_copy(meta, meta_ref, csem)
+    keep.start()
     slots = lax.broadcasted_iota(jnp.int32, (cap, t), 0).astype(F32)
 
     def build(s, _):
-        parts = []
         for e in range(el):
             sel = meta[s, e:e + 1, :] == slots
             disp[s, e * cap:(e + 1) * cap, :] = jnp.where(sel, 1.0, 0.0).astype(BF)
-            parts.append(jnp.where(sel, meta[s, el + e:el + e + 1, :], 0.0))
-        w = jnp.concatenate(parts, axis=0).T
-        n = el * cap
-        slot = lax.rem(s, 2)
-
-        @pl.when(s >= 2)
-        def _():
-            pltpu.make_async_copy(wst.at[slot], wc_ref.at[s - 2], csem.at[slot]).wait()
-
-        for i in range(3):
-            p = w.astype(BF)
-            wst[slot, :, i * n:(i + 1) * n] = p
-            w = w - p.astype(F32)
-        pltpu.make_async_copy(wst.at[slot], wc_ref.at[s], csem.at[slot]).start()
         return 0
 
     lax.fori_loop(0, 8, build, 0)
@@ -209,14 +198,25 @@
 
         lax.fori_loop(0, 8, body, 0)
 
-    def product(k, e):
+    def product(k, e, use):
         b = nsh + k * el + e
         fetch(b + NS - 1)
         ready(b)
-        return jnp.dot(xe[e].reshape(8 * cap, kw), wb[lax.rem(b, NS)], preferred_element_type=F32)
+        slot = lax.rem(b, NS)
+        u = xe[e].reshape(8 * cap, kw)
+
+        def part(at):
+            return jnp.dot(u, wb[slot, :, at], preferred_element_type=F32)
+        use(part)
+
+    def slabs(w):
+        return [slice(i, min(i + w, 2 * f)) for i in range(0, 2 * f, w)]
 
     def start_acc(e, _):
-        acc[e] = product(0, e)
+        def use(part):
+            for at in slabs(SLAB):
+                acc[e, :, at] = part(at)
+        product(0, e, use)
         return 0
 
     corner(0)
@@ -232,7 +232,10 @@
         gather(k)
 
         def add(e, _):
-            acc[e] += product(k, e)
+            def use(part):
+                for at in slabs(SLAB):
+                    acc[e, :, at] += part(at)
+            product(k, e, use)
             return 0
 
         lax.fori_loop(0, el // 2, add, 0)
@@ -253,19 +256,34 @@
 
     def last(e, _):
         slot = lax.rem(e, 2)
-        acc[e] += product(NK - 1, e)
 
         @pl.when(e >= 2)
         def _():
             pltpu.make_async_copy(hst.at[slot], h_ref.at[e - 2], osem.at[slot]).wait()
-        hst[slot] = silu_mul(acc[e, :, 0:f], acc[e, :, f:2 * f])
+
+        def use(part):
+            nt = f // 128
+            live = {}
+            order = [nt // 2] + [v for i in range(nt // 2) for v in (i, nt // 2 + 1 + i)]
+            for i in order:
+                at = slice(i * 256, i * 256 + 256)
+                d = acc[e, :, at] + part(at)
+                for j in (2 * i, 2 * i + 1):
+                    live[j] = d[:, (j - 2 * i) * 128:(j - 2 * i) * 128 + 128]
+                    if j == nt - 1:
+                        acc[e, :, j * 128:j * 128 + 128] = live.pop(j)
+                for j in [v for v in live if v < nt and v + nt in live]:
+                    hst[slot, :, j * 128:j * 128 + 128] = silu_mul(live.pop(j), live.pop(j + nt))
+                if 2 * nt - 1 in live:
+                    j = nt - 1
+                    hst[slot, :, j * 128:j * 128 + 128] = silu_mul(acc[e, :, j * 128:j * 128 + 128], live.pop(2 * nt - 1))
+        product(NK - 1, e, use)
         pltpu.make_async_copy(hst.at[slot], h_ref.at[e], osem.at[slot]).start()
         return 0
 
     lax.fori_loop(0, el, last, 0)
 
-    for s in (6, 7):
-        pltpu.make_async_copy(wst.at[s % 2], wc_ref.at[s], csem.at[s % 2]).wait()
+    keep.wait()
     for e in (el - 2, el - 1):
         pltpu.make_async_copy(hst.at[e % 2], h_ref.at[e], osem.at[e % 2]).wait()
     for o in others:
@@ -274,8 +292,8 @@
         sent(k)
 
 
-def second(el, cap, h_ref, sh_ref, wc_ref, x_ref, w2_ref, ws2_ref, y_ref,
-           hv, shv, wcv, xv, wb, o3, part, pr, dr, fr, res, yst,
+def second(el, cap, h_ref, sh_ref, meta_ref, x_ref, w2_ref, ws2_ref, y_ref,
+           hv, shv, wcv, meta, xv, wb, o3, part, pr, dr, fr, res, yst,
            hsem, csem, xsem, wsem, ysem, psend, precv, dsend, drecv, fsend, frecv):
     ey, ex, ec, dev, chip = place()
     t, hd = x_ref.shape
@@ -316,7 +334,9 @@
     for e in range(1, el):
         hcopy(e).start()
     loads = [pltpu.make_async_copy(sh_ref, shv, xsem.at[0]), pltpu.make_async_copy(x_ref, xv, xsem.at[1]),
-             pltpu.make_async_copy(wc_ref, wcv, csem)]
+             ]
+    m = pltpu.make_async_copy(meta_ref, meta, csem)
+    m.start()
     for c in loads:
         c.start()
 
@@ -324,6 +344,20 @@
     for to in "xyp":
         pl.semaphore_signal(barrier, inc=1, device_id=dev[to], device_id_type=MESH)
     pl.semaphore_wait(barrier, 3)
+
+    m.wait()
+    slots = lax.broadcasted_iota(jnp.int32, (cap, t), 0).astype(F32)
+
+    def build(s, _):
+        parts = [jnp.where(meta[s, e:e + 1, :] == slots, meta[s, el + e:el + e + 1, :], 0.0) for e in range(el)]
+        w = jnp.concatenate(parts, axis=0).T
+        for i in range(3):
+            p = w.astype(BF)
+            wcv[s, :, i * n:(i + 1) * n] = p
+            w = w - p.astype(F32)
+        return 0
+
+    lax.fori_loop(0, 8, build, 0)
 
     def swap(c):
         return pltpu.make_async_remote_copy(part.at[1, c], pr.at[c], psend.at[c], precv.at[c], device_id=dev["p"],
@@ -366,13 +400,15 @@
 
         lax.fori_loop(0, el, expert, 0)
 
-        @pl.when(c == 0)
-        def _():
-            for d in loads:
-                d.wait()
         weigh(c, 1)
         swap(c).start()
         weigh(c, 0)
+
+    def shared(c):
+        @pl.when(c == 0)
+        def _():
+            for d in loads:
+                d.wait()
         s = None
         for i in range(2):
             b = c * per + el + i
@@ -420,17 +456,18 @@
         def _():
             compute(c)
             stage1(c)
+            shared(c)
 
         @pl.when((c >= 1) & (c < nc + 1))
         def _():
             stage2(c - 1)
 
-        @pl.when(c >= 2)
-        def _():
-            stage3(c - 2)
-        return 0
-
-    lax.fori_loop(0, nc + 2, step, 0)
+        @pl.when(c >= LAG)
+        def _():
+            stage3(c - LAG)
+        return 0
+
+    lax.fori_loop(0, nc + LAG, step, 0)
     for c in (nc - 2, nc - 1):
         ycopy(c).wait()
 
@@ -457,34 +494,32 @@
         n = el * cap
         kw = hd // NK
         nc = hd // CW
-        idt = jnp.pad(ids.T, ((0, 8 - top), (0, 0)), constant_values=-1)
-        gt = jnp.pad(gates.T, ((0, 8 - top), (0, 0)))
         dma = pltpu.SemaphoreType.DMA
-        h, sh, wc = pl.pallas_call(
+        h, sh, meta = pl.pallas_call(
             functools.partial(first, el, cap),
             out_shape=(jax.ShapeDtypeStruct((el, pg * cap, f), BF), jax.ShapeDtypeStruct((2, t, f), BF),
-                       jax.ShapeDtypeStruct((pg, t, 3 * n), BF)),
+                       jax.ShapeDtypeStruct((pg, 2 * el, t), F32)),
             in_specs=[VM, VM] + [ANY] * 5, out_specs=(ANY,) * 3,
             scratch_shapes=[
                 pltpu.VMEM((NK, pg, t, kw), BF), pltpu.VMEM((el, pg * cap, 2 * f), F32), pltpu.VMEM((NS, kw, 2 * f), BF),
                 pltpu.VMEM((pg, n, t), BF), pltpu.VMEM((el, pg, cap, kw), BF), pltpu.VMEM((2, pg * cap, f), BF),
-                pltpu.VMEM((2, t, 3 * n), BF), pltpu.VMEM((pg, 2 * el, t), F32), pltpu.VMEM((pg, 2 * el, t), F32),
-                dma((NK,)), dma((NS, 2)), dma((2,)), dma((2,)), dma((8,)), dma((8,)), dma((NK, 9)), dma((NK, 9))],
+                pltpu.VMEM((pg, 2 * el, t), F32), pltpu.VMEM((pg, 2 * el, t), F32),
+                dma((NK,)), dma((NS, 2)), dma((2,)), dma, dma((8,)), dma((8,)), dma((NK, 9)), dma((NK, 9))],
             compiler_params=pltpu.CompilerParams(collective_id=0, has_side_effects=True, vmem_limit_bytes=VLIM),
-        )(idt, gt, x, w1, w3, ws1, ws3)
+        )(ids.T, gates.T, x, w1, w3, ws1, ws3)
         return pl.pallas_call(
             functools.partial(second, el, cap),
             out_shape=jax.ShapeDtypeStruct((t, hd), BF),
             in_specs=[ANY] * 6, out_specs=ANY,
             scratch_shapes=[
-                pltpu.VMEM((el, pg * cap, f), BF), pltpu.VMEM((2, t, f), BF), pltpu.VMEM((pg, t, 3 * n), BF),
+                pltpu.VMEM((el, pg * cap, f), BF), pltpu.VMEM((2, t, f), BF), pltpu.VMEM((pg, t, 3 * n), BF), pltpu.VMEM((pg, 2 * el, t), F32),
                 pltpu.VMEM((t, hd), BF), pltpu.VMEM((NW, f, CW), BF), pltpu.VMEM((pg, 3 * n, CW), BF),
                 pltpu.VMEM((2, nc, 4, t, CW), F32), pltpu.VMEM((nc, 4, t, CW), F32), pltpu.VMEM((nc, 2, t // 2, CW), F32),
                 pltpu.VMEM((nc, 2, t, CW), F32), pltpu.VMEM((nc, t, CW), F32), pltpu.VMEM((2, t, CW), BF),
                 dma((el,)), dma, dma((2,)), dma((NW,)), dma((2,)), dma((nc,)), dma((nc,)), dma((nc, 2)), dma((nc, 2)),
                 dma((nc, 2, 2)), dma((nc, 2, 2))],
             compiler_params=pltpu.CompilerParams(collective_id=1, has_side_effects=True, vmem_limit_bytes=VLIM),
-        )(h, sh, wc, x, w2, ws2)
+        )(h, sh, meta, x, w2, ws2)
 
     return jax.shard_map(local, mesh=mesh,
                          in_specs=(P(ALL), P(ALL), P(ALL), P(EXP), P(EXP), P(EXP), P(), P(), P()),

time: 184 us -> 171 us (0.929)
  Pallas kernels: 179 us -> 168 us
  local copies, waits for them, and re-layouts: 4.9 us -> 2.3 us
    pallas_call x1, Pallas kernels: 86.9 us -> 78 us  [local(): pl.pallas_call(functools.partial(first, el, cap), out_shape=(jax.ShapeDty...]
    pad x2 -> x0, local copies, waits for them, and re-layouts: 2.59 us -> none  [the longest x1 1.3 us: local(): idt = jnp.pad(ids.T, ((0, 8 - top), (0, 0)), constant_values=-1)]
    pallas_call x1, Pallas kernels: 92.2 us -> 90.3 us  [local(): pl.pallas_call(functools.partial(second, el, cap), out_shape=jax.ShapeDty...]
where the time goes in v4:
time: 171 us
  Pallas kernels  168 us (98%)
  local copies, waits for them, and re-layouts  2.3 us (1%)
    pallas_call x1, Pallas kernels, local(): pl.pallas_call(functools.partial(second, el, cap), out_shape=jax.ShapeDty...  90.3 us
    pallas_call x1, Pallas kernels, local(): pl.pallas_call(functools.partial(first, el, cap), out_shape=(jax.ShapeDty...  78 us

profile of v4, /device:TPU:0, one launch (start us, length us, event | category | flops | bytes accessed | tf_op | source)
XLA Modules:
  0.0 170.5 jit_solution(2260145786119306735)
XLA Ops:
  0.0 78.0 %shard_map.91 = (bf16[8,384,1408]{2,1,0:T(8,128)(2,1)}, bf16[2,256,1408]{2,1,0:T(8,128)(2,1)}, f32[8,16,256]{2,1,0:T(8,128)}) custom-call(s32[6,256]{1,0:T(8,128)} %bitcast.2, f32[6,256]{1,0:T(8,128)} %bitcast.3, bf16[256,2048]{1,0:T(8,128)(2,1)} %x_ref.3, bf16[8,2048,1408]{2,1,0:T(8,128)(2,1)} %w1_ref.1, bf16[8,2048,1408]{2,1,0:T(8,128)(2,1)} %w3_ref.1, ...), custom_call_target="tpu_custom_call" | custom-call | tf_op jit(solution)/shard_map/pallas_call | solution.py:498
  78.0 90.3 %shard_map.92 = bf16[256,2048]{1,0:T(8,128)(2,1)} custom-call(bf16[8,384,1408]{2,1,0:T(8,128)(2,1)} %get-tuple-element.8.h_ref, bf16[2,256,1408]{2,1,0:T(8,128)(2,1)} %get-tuple-element.9.sh_ref, f32[8,16,256]{2,1,0:T(8,128)} %get-tuple-element.10.meta_ref, bf16[256,2048]{1,0:T(8,128)(2,1)} %x_ref.3, bf16[8,1408,2048]{2,1,0:T(8,128)(2,1)} %w2_ref.1, ...), custom_call_target="tpu_custom_call" | custom-call | tf_op jit(solution)/shard_map/pallas_call | solution.py:510
  168.2 2.3 %copy.11 = bf16[256,2048]{1,0:T(8,128)(2,1)} copy(bf16[256,2048]{1,0:T(8,128)(2,1)} %shard_map.92) | data formatting | bytes 2097152

commit v5 on v4

--- a/solution.py
+++ b/solution.py
@@ -17,9 +17,9 @@
 VLIM = 67043328
 
 NK = 4
-NS = 3
+NS = 4
 CW = 256
-NW = 4
+NW = 12
 LAG = 3
 SLAB = 256
 
@@ -153,7 +153,6 @@
     for o in others:
         mcopy(o).start()
     direct(0)
-    direct(1)
 
     for hf in range(2):
         acc[0, 0:t, :] = jnp.zeros((t, 2 * f), F32)
@@ -168,9 +167,10 @@
         lax.fori_loop(0, NK, body, 0)
         hst[hf, 0:t, :] = silu_mul(acc[0, 0:t, 0:f], acc[0, 0:t, f:2 * f])
         pltpu.make_async_copy(hst.at[hf, 0:t], sh_ref.at[hf], osem.at[hf]).start()
-
-    relay(0)
-    direct(2)
+        if hf == 0:
+            relay(0)
+            direct(1)
+
 
     meta[mine["o"]] = mout[ey * 4 + ex * 2 + ec]
     for o in others:
@@ -186,8 +186,6 @@
         return 0
 
     lax.fori_loop(0, 8, build, 0)
-    relay(1)
-    direct(3)
 
     def gather(k):
         def body(s, _):
@@ -222,10 +220,12 @@
     corner(0)
     arrived(0)
     gather(0)
-    lax.fori_loop(0, el // 2, start_acc, 0)
-    relay(2)
+    lax.fori_loop(0, el // 4, start_acc, 0)
+    relay(1)
+    direct(2)
+    lax.fori_loop(el // 4, el - el // 4, start_acc, 0)
     corner(1)
-    lax.fori_loop(el // 2, el, start_acc, 0)
+    lax.fori_loop(el - el // 4, el, start_acc, 0)
 
     def more(k, _):
         arrived(k)
@@ -238,13 +238,15 @@
             product(k, e, use)
             return 0
 
-        lax.fori_loop(0, el // 2, add, 0)
-
-        @pl.when(k == 1)
-        def _():
-            relay(3)
+        lax.fori_loop(0, el // 4, add, 0)
+        relay(k + 1)
+
+        @pl.when(k < NK - 2)
+        def _():
+            direct(k + 2)
+        lax.fori_loop(el // 4, el - el // 4, add, 0)
         corner(k + 1)
-        lax.fori_loop(el // 2, el, add, 0)
+        lax.fori_loop(el - el // 4, el, add, 0)
         return 0
 
     lax.fori_loop(1, NK - 1, more, 0)
@@ -455,8 +457,8 @@
         @pl.when(c < nc)
         def _():
             compute(c)
+            shared(c)
             stage1(c)
-            shared(c)
 
         @pl.when((c >= 1) & (c < nc + 1))
         def _():

time: 171 us -> 167 us (0.977)
  Pallas kernels: 168 us -> 165 us
    pallas_call x1, Pallas kernels: 78 us -> 74.3 us  [local(): pl.pallas_call(functools.partial(first, el, cap), out_shape=(jax.ShapeDty...]
where the time goes in v5:
time: 167 us
  Pallas kernels  165 us (99%)
  local copies, waits for them, and re-layouts  2.3 us (1%)
    pallas_call x1, Pallas kernels, local(): pl.pallas_call(functools.partial(second, el, cap), out_shape=jax.ShapeDty...  90.3 us
    pallas_call x1, Pallas kernels, local(): pl.pallas_call(functools.partial(first, el, cap), out_shape=(jax.ShapeDty...  74.3 us

profile of v5, /device:TPU:0, one launch (start us, length us, event | category | flops | bytes accessed | tf_op | source)
XLA Modules:
  0.0 167.0 jit_solution(1301360650564018111)
XLA Ops:
  0.0 74.3 %shard_map.91 = (bf16[8,384,1408]{2,1,0:T(8,128)(2,1)}, bf16[2,256,1408]{2,1,0:T(8,128)(2,1)}, f32[8,16,256]{2,1,0:T(8,128)}) custom-call(s32[6,256]{1,0:T(8,128)} %bitcast.2, f32[6,256]{1,0:T(8,128)} %bitcast.3, bf16[256,2048]{1,0:T(8,128)(2,1)} %x_ref.3, bf16[8,2048,1408]{2,1,0:T(8,128)(2,1)} %w1_ref.1, bf16[8,2048,1408]{2,1,0:T(8,128)(2,1)} %w3_ref.1, ...), custom_call_target="tpu_custom_call" | custom-call | tf_op jit(solution)/shard_map/pallas_call | solution.py:500
  74.3 90.3 %shard_map.92 = bf16[256,2048]{1,0:T(8,128)(2,1)} custom-call(bf16[8,384,1408]{2,1,0:T(8,128)(2,1)} %get-tuple-element.8.h_ref, bf16[2,256,1408]{2,1,0:T(8,128)(2,1)} %get-tuple-element.9.sh_ref, f32[8,16,256]{2,1,0:T(8,128)} %get-tuple-element.10.meta_ref, bf16[256,2048]{1,0:T(8,128)(2,1)} %x_ref.3, bf16[8,1408,2048]{2,1,0:T(8,128)(2,1)} %w2_ref.1, ...), custom_call_target="tpu_custom_call" | custom-call | tf_op jit(solution)/shard_map/pallas_call | solution.py:512
  164.7 2.3 %copy.11 = bf16[256,2048]{1,0:T(8,128)(2,1)} copy(bf16[256,2048]{1,0:T(8,128)(2,1)} %shard_map.92) | data formatting | bytes 2097152

commit v6 on v5

--- a/solution.py
+++ b/solution.py
@@ -17,10 +17,9 @@
 VLIM = 67043328
 
 NK = 4
-NS = 4
+NS = 5
 CW = 256
-NW = 12
-LAG = 3
+NW = 8
 SLAB = 256
 
 
@@ -72,7 +71,13 @@
     def ready(b):
         block(b, lambda c: c.wait())
 
-    for b in range(NS - 1):
+    def pair(b):
+        for j in range(2):
+            fetch(b + NS - 2 + j)
+        for j in range(2):
+            ready(b + j)
+
+    for b in range(NS - 2):
         fetch(b)
     for k in range(NK):
         pltpu.make_async_copy(x_ref.at[:, pl.ds(k * kw, kw)], xg.at[k, mine["o"]], xsem.at[k]).start()
@@ -157,15 +162,18 @@
     for hf in range(2):
         acc[0, 0:t, :] = jnp.zeros((t, 2 * f), F32)
 
-        def body(k, _):
-            b = hf * NK + k
-            fetch(b + NS - 1)
-            ready(b)
-            acc[0, 0:t, :] += jnp.dot(xg[k, mine["o"]], wb[lax.rem(b, NS)], preferred_element_type=F32)
+        def body(i, _):
+            b = hf * NK + 2 * i
+            pair(b)
+            for at in [slice(v, v + SLAB) for v in range(0, 2 * f, SLAB)]:
+                d = [jnp.dot(xg[2 * i + j, mine["o"]], wb[lax.rem(b + j, NS), :, at], preferred_element_type=F32)
+                     for j in range(2)]
+                acc[0, 0:t, at] += d[0] + d[1]
             return 0
 
-        lax.fori_loop(0, NK, body, 0)
-        hst[hf, 0:t, :] = silu_mul(acc[0, 0:t, 0:f], acc[0, 0:t, f:2 * f])
+        lax.fori_loop(0, NK // 2, body, 0)
+        for v in range(0, f, 128):
+            hst[hf, 0:t, v:v + 128] = silu_mul(acc[0, 0:t, v:v + 128], acc[0, 0:t, f + v:f + v + 128])
         pltpu.make_async_copy(hst.at[hf, 0:t], sh_ref.at[hf], osem.at[hf]).start()
         if hf == 0:
             relay(0)
@@ -196,57 +204,54 @@
 
         lax.fori_loop(0, 8, body, 0)
 
-    def product(k, e, use):
-        b = nsh + k * el + e
-        fetch(b + NS - 1)
-        ready(b)
-        slot = lax.rem(b, NS)
-        u = xe[e].reshape(8 * cap, kw)
-
-        def part(at):
-            return jnp.dot(u, wb[slot, :, at], preferred_element_type=F32)
-        use(part)
+    def products(k, i, use):
+        b = nsh + k * el + 2 * i
+        pair(b)
+        for j in range(2):
+            slot = lax.rem(b + j, NS)
+            u = xe[2 * i + j].reshape(8 * cap, kw)
+            use(2 * i + j, lambda at, u=u, slot=slot: jnp.dot(u, wb[slot, :, at], preferred_element_type=F32))
 
     def slabs(w):
         return [slice(i, min(i + w, 2 * f)) for i in range(0, 2 * f, w)]
 
-    def start_acc(e, _):
-        def use(part):
+    def start_acc(i, _):
+        def use(e, part):
             for at in slabs(SLAB):
                 acc[e, :, at] = part(at)
-        product(0, e, use)
+        products(0, i, use)
         return 0
 
     corner(0)
     arrived(0)
     gather(0)
-    lax.fori_loop(0, el // 4, start_acc, 0)
+    lax.fori_loop(0, el // 8, start_acc, 0)
     relay(1)
     direct(2)
-    lax.fori_loop(el // 4, el - el // 4, start_acc, 0)
+    lax.fori_loop(el // 8, el // 2 - el // 8, start_acc, 0)
     corner(1)
-    lax.fori_loop(el - el // 4, el, start_acc, 0)
+    lax.fori_loop(el // 2 - el // 8, el // 2, start_acc, 0)
 
     def more(k, _):
         arrived(k)
         gather(k)
 
-        def add(e, _):
-            def use(part):
+        def add(i, _):
+            def use(e, part):
                 for at in slabs(SLAB):
                     acc[e, :, at] += part(at)
-            product(k, e, use)
+            products(k, i, use)
             return 0
 
-        lax.fori_loop(0, el // 4, add, 0)
+        lax.fori_loop(0, el // 8, add, 0)
         relay(k + 1)
 
         @pl.when(k < NK - 2)
         def _():
             direct(k + 2)
-        lax.fori_loop(el // 4, el - el // 4, add, 0)
+        lax.fori_loop(el // 8, el // 2 - el // 8, add, 0)
         corner(k + 1)
-        lax.fori_loop(el - el // 4, el, add, 0)
+        lax.fori_loop(el // 2 - el // 8, el // 2, add, 0)
         return 0
 
     lax.fori_loop(1, NK - 1, more, 0)
@@ -256,14 +261,14 @@
     for hf in range(2):
         pltpu.make_async_copy(hst.at[hf, 0:t], sh_ref.at[hf], osem.at[hf]).wait()
 
-    def last(e, _):
-        slot = lax.rem(e, 2)
-
-        @pl.when(e >= 2)
-        def _():
-            pltpu.make_async_copy(hst.at[slot], h_ref.at[e - 2], osem.at[slot]).wait()
-
-        def use(part):
+    def last(i, _):
+        @pl.when(i >= 1)
+        def _():
+            for j in range(2):
+                pltpu.make_async_copy(hst.at[j], h_ref.at[2 * i - 2 + j], osem.at[j]).wait()
+
+        def use(e, part):
+            slot = lax.rem(e, 2)
             nt = f // 128
             live = {}
             order = [nt // 2] + [v for i in range(nt // 2) for v in (i, nt // 2 + 1 + i)]
@@ -279,11 +284,11 @@
                 if 2 * nt - 1 in live:
                     j = nt - 1
                     hst[slot, :, j * 128:j * 128 + 128] = silu_mul(acc[e, :, j * 128:j * 128 + 128], live.pop(2 * nt - 1))
-        product(NK - 1, e, use)
-        pltpu.make_async_copy(hst.at[slot], h_ref.at[e], osem.at[slot]).start()
-        return 0
-
-    lax.fori_loop(0, el, last, 0)
+            pltpu.make_async_copy(hst.at[slot], h_ref.at[e], osem.at[slot]).start()
+        products(NK - 1, i, use)
+        return 0
+
+    lax.fori_loop(0, el // 2, last, 0)
 
     keep.wait()
     for e in (el - 2, el - 1):
@@ -295,8 +300,8 @@
 
 
 def second(el, cap, h_ref, sh_ref, meta_ref, x_ref, w2_ref, ws2_ref, y_ref,
-           hv, shv, wcv, meta, xv, wb, o3, part, pr, dr, fr, res, yst,
-           hsem, csem, xsem, wsem, ysem, psend, precv, dsend, drecv, fsend, frecv):
+           hv, shv, wcv, meta, xv, wb, o3, part, give, pr, sb, rv, res, yst,
+           hsem, csem, xsem, wsem, ysem, psend, precv, ssem, rsem, esend, erecv):
     ey, ex, ec, dev, chip = place()
     t, hd = x_ref.shape
     nc = hd // CW
@@ -339,8 +344,6 @@
              ]
     m = pltpu.make_async_copy(meta_ref, meta, csem)
     m.start()
-    for c in loads:
-        c.start()
 
     barrier = pltpu.get_barrier_semaphore()
     for to in "xyp":
@@ -361,29 +364,26 @@
 
     lax.fori_loop(0, 8, build, 0)
 
-    def swap(c):
-        return pltpu.make_async_remote_copy(part.at[1, c], pr.at[c], psend.at[c], precv.at[c], device_id=dev["p"],
+    def swap(c, i):
+        ch = chip["dxyo"[i]]
+        return pltpu.make_async_remote_copy(give.at[lax.rem(c, 2), ch], pr.at[c, ch], psend.at[c, i], precv.at[c, i],
+                                            device_id=dev["p"], device_id_type=MESH)
+
+    def ship(c, i, a, b, k=None):
+        send, recv = (ssem.at[c, i], rsem.at[c, i]) if k is None else (esend.at[k, i], erecv.at[k, i])
+        at = pl.ds(a, b - a)
+        return pltpu.make_async_remote_copy(sb.at[i, c, at], rv.at[i, c, at], send, recv, device_id=dev["xy"[i]],
                                             device_id_type=MESH)
 
-    def corner(c, i):
-        src = part.at[0, c, chip["d"], (lo, hi)[i]]
-        return pltpu.make_async_remote_copy(src, dr.at[c, i], dsend.at[c, i], drecv.at[c, i], device_id=dev["xy"[i]],
-                                            device_id_type=MESH)
-
-    def final(c, i, rows):
-        src = part.at[0, c, chip["xy"[i]], (lo, hi)[rows]]
-        return pltpu.make_async_remote_copy(src, fr.at[c, i, (lo, hi)[rows]], fsend.at[c, i, rows], frecv.at[c, i, rows],
-                                            device_id=dev["xy"[i]], device_id_type=MESH)
-
-    def weigh(c, g):
-        core = ec if g == 0 else 1 - ec
-
-        def body(ch, _):
-            s = core * 4 + ch
-            part[g, c, ch] = jnp.dot(wcv[s], o3[s], preferred_element_type=F32)
-            return 0
-
-        lax.fori_loop(0, 4, body, 0)
+    def dispatch(c, op):
+        for i in range(2):
+            pl.when(c < 2)(lambda: op(ship(c, i, 0, 2)))
+            pl.when((c >= 2) & (c < nc - 1))(lambda: op(ship(c, i, 0, 3)))
+            pl.when(c == nc - 1)(lambda: op(ship(c, i, 0, 1)))
+
+    def weigh(c, ch, core):
+        s = core * 4 + chip[ch]
+        return jnp.dot(wcv[s], o3[s], preferred_element_type=F32)
 
     def compute(c):
         def expert(e, _):
@@ -402,9 +402,20 @@
 
         lax.fori_loop(0, el, expert, 0)
 
-        weigh(c, 1)
-        swap(c).start()
-        weigh(c, 0)
+        @pl.when(c == 0)
+        def _():
+            for d in loads:
+                d.start()
+
+        @pl.when(c >= 2)
+        def _():
+            for i in range(4):
+                swap(c - 2, i).wait_send()
+        for i, ch in enumerate("dxyo"):
+            give[lax.rem(c, 2), chip[ch]] = weigh(c, ch, 1 - ec)
+            swap(c, i).start()
+        for ch in "dxyo":
+            part[c, chip[ch]] = weigh(c, ch, ec)
 
     def shared(c):
         @pl.when(c == 0)
@@ -422,63 +433,89 @@
         res[c] = xv[:, cols].astype(F32) + s.astype(BF).astype(F32)
 
     def stage1(c):
-        swap(c).wait_recv()
-        for ch in "dxyo":
-            part[0, c, chip[ch]] += pr[c, chip[ch]]
-        corner(c, 0).start()
-        corner(c, 1).start()
-        final(c, 0, 0).start()
-        final(c, 1, 1).start()
-
-    def stage2(c):
-        corner(c, 0).wait_recv()
-        part[0, c, chip["y"], 0:half] += dr[c, 0]
-        corner(c, 1).wait_recv()
-        part[0, c, chip["x"], half:t] += dr[c, 1]
-        final(c, 1, 0).start()
-        final(c, 0, 1).start()
+        d, x, y, o = (chip[ch] for ch in "dxyo")
+        swap(c, 0).wait_recv()
+        sb[0, c, 0] = part[c, d, 0:half] + pr[c, d, 0:half]
+        sb[1, c, 0] = part[c, d, half:t] + pr[c, d, half:t]
+        swap(c, 1).wait_recv()
+        sb[0, c, 1] = part[c, x, 0:half] + pr[c, x, 0:half]
+        part[c, x, half:t] += pr[c, x, half:t]
+        swap(c, 2).wait_recv()
+        part[c, y, 0:half] += pr[c, y, 0:half]
+        sb[1, c, 1] = part[c, y, half:t] + pr[c, y, half:t]
+        swap(c, 3).wait_recv()
+        part[c, o] += pr[c, o]
+
+    def stage2(c, into):
+        sb[1, into, 2] = part[c, chip["y"], 0:half] + rv[0, c, 0]
+        sb[0, into, 2] = part[c, chip["x"], half:t] + rv[1, c, 0]
 
     def ycopy(c):
         cols = pl.ds(pl.multiple_of(c * CW, CW), CW)
         return pltpu.make_async_copy(yst.at[lax.rem(c, 2)], y_ref.at[:, cols], ysem.at[lax.rem(c, 2)])
 
     def stage3(c):
+        n2 = lax.rem(c + 2, nc)
+
+        @pl.when(c >= 2)
+        def _():
+            ycopy(c - 2).wait()
+        own = res[c] + part[c, chip["o"]]
+        yst[lax.rem(c, 2), 0:half] = (own[0:half] + rv[0, c, 1] + rv[1, n2, 2]).astype(BF)
+        yst[lax.rem(c, 2), half:t] = (own[half:t] + rv[0, n2, 2] + rv[1, c, 1]).astype(BF)
+        ycopy(c).start()
+
+    def step(c, _):
+        compute(c)
+
+        @pl.when(c >= 2)
+        def _():
+            dispatch(c - 2, lambda d: d.wait_recv())
+            stage2(c - 2, c)
+        stage1(c)
+        dispatch(c, lambda d: d.start())
+
+        @pl.when(c == nc - 1)
+        def _():
+            for i in range(2):
+                ship(nc - 1, i, 1, 3, 0).start()
+        shared(c)
+
+        @pl.when(c >= 4)
+        def _():
+            stage3(c - 4)
+        return 0
+
+    lax.fori_loop(0, nc, step, 0)
+    for i in range(2):
+        ship(nc - 2, i, 0, 3).wait_recv()
+    stage2(nc - 2, 0)
+    for i in range(2):
+        ship(0, i, 2, 3, 1).start()
+    stage3(nc - 4)
+    for i in range(2):
+        ship(nc - 1, i, 0, 1).wait_recv()
+    stage2(nc - 1, 1)
+    for i in range(2):
+        ship(1, i, 2, 3, 2).start()
+    for i in range(2):
+        ship(nc - 1, i, 1, 3, 0).wait_recv()
+    stage3(nc - 3)
+    for k in range(2):
         for i in range(2):
-            for rows in range(2):
-                final(c, i, rows).wait_recv()
-
-        @pl.when(c >= 2)
-        def _():
-            ycopy(c - 2).wait()
-        yst[lax.rem(c, 2)] = (res[c] + (part[0, c, chip["o"]] + fr[c, 0] + fr[c, 1])).astype(BF)
-        ycopy(c).start()
-
-    def step(c, _):
-        @pl.when(c < nc)
-        def _():
-            compute(c)
-            shared(c)
-            stage1(c)
-
-        @pl.when((c >= 1) & (c < nc + 1))
-        def _():
-            stage2(c - 1)
-
-        @pl.when(c >= LAG)
-        def _():
-            stage3(c - LAG)
-        return 0
-
-    lax.fori_loop(0, nc + LAG, step, 0)
+            ship(k, i, 2, 3, k + 1).wait_recv()
+        stage3(nc - 2 + k)
     for c in (nc - 2, nc - 1):
         ycopy(c).wait()
+        for i in range(4):
+            swap(c, i).wait_send()
+    for i in range(2):
+        ship(nc - 1, i, 1, 3, 0).wait_send()
+        for k in range(2):
+            ship(k, i, 2, 3, k + 1).wait_send()
 
     def drain(c, _):
-        swap(c).wait_send()
-        for i in range(2):
-            corner(c, i).wait_send()
-            for rows in range(2):
-                final(c, i, rows).wait_send()
+        dispatch(c, lambda d: d.wait_send())
         return 0
 
     lax.fori_loop(0, nc, drain, 0)
@@ -516,10 +553,11 @@
             scratch_shapes=[
                 pltpu.VMEM((el, pg * cap, f), BF), pltpu.VMEM((2, t, f), BF), pltpu.VMEM((pg, t, 3 * n), BF), pltpu.VMEM((pg, 2 * el, t), F32),
                 pltpu.VMEM((t, hd), BF), pltpu.VMEM((NW, f, CW), BF), pltpu.VMEM((pg, 3 * n, CW), BF),
-                pltpu.VMEM((2, nc, 4, t, CW), F32), pltpu.VMEM((nc, 4, t, CW), F32), pltpu.VMEM((nc, 2, t // 2, CW), F32),
-                pltpu.VMEM((nc, 2, t, CW), F32), pltpu.VMEM((nc, t, CW), F32), pltpu.VMEM((2, t, CW), BF),
-                dma((el,)), dma, dma((2,)), dma((NW,)), dma((2,)), dma((nc,)), dma((nc,)), dma((nc, 2)), dma((nc, 2)),
-                dma((nc, 2, 2)), dma((nc, 2, 2))],
+                pltpu.VMEM((nc, 4, t, CW), F32), pltpu.VMEM((2, 4, t, CW), F32), pltpu.VMEM((nc, 4, t, CW), F32),
+                pltpu.VMEM((2, nc, 3, t // 2, CW), F32), pltpu.VMEM((2, nc, 3, t // 2, CW), F32),
+                pltpu.VMEM((nc, t, CW), F32), pltpu.VMEM((2, t, CW), BF),
+                dma((el,)), dma, dma((2,)), dma((NW,)), dma((2,)), dma((nc, 4)), dma((nc, 4)), dma((nc, 2)), dma((nc, 2)),
+                dma((3, 2)), dma((3, 2))],
             compiler_params=pltpu.CompilerParams(collective_id=1, has_side_effects=True, vmem_limit_bytes=VLIM),
         )(h, sh, meta, x, w2, ws2)
 

time: 167 us -> 168 us (level)
  no operation moved by 1% of the time
where the time goes in v6:
time: 168 us
  Pallas kernels  166 us (99%)
  local copies, waits for them, and re-layouts  2.3 us (1%)
    pallas_call x1, Pallas kernels, local(): pl.pallas_call(functools.partial(second, el, cap), out_shape=jax.ShapeDty...  91 us
    pallas_call x1, Pallas kernels, local(): pl.pallas_call(functools.partial(first, el, cap), out_shape=(jax.ShapeDty...  74.6 us

profile of v6, /device:TPU:0, one launch (start us, length us, event | category | flops | bytes accessed | tf_op | source)
XLA Modules:
  0.0 167.9 jit_solution(2980806151803998969)
XLA Ops:
  0.0 74.6 %shard_map.91 = (bf16[8,384,1408]{2,1,0:T(8,128)(2,1)}, bf16[2,256,1408]{2,1,0:T(8,128)(2,1)}, f32[8,16,256]{2,1,0:T(8,128)}) custom-call(s32[6,256]{1,0:T(8,128)} %bitcast.2, f32[6,256]{1,0:T(8,128)} %bitcast.3, bf16[256,2048]{1,0:T(8,128)(2,1)} %x_ref.3, bf16[8,2048,1408]{2,1,0:T(8,128)(2,1)} %w1_ref.1, bf16[8,2048,1408]{2,1,0:T(8,128)(2,1)} %w3_ref.1, ...), custom_call_target="tpu_custom_call" | custom-call | tf_op jit(solution)/shard_map/pallas_call | solution.py:537
  74.6 91.0 %shard_map.92 = bf16[256,2048]{1,0:T(8,128)(2,1)} custom-call(bf16[8,384,1408]{2,1,0:T(8,128)(2,1)} %get-tuple-element.8.h_ref, bf16[2,256,1408]{2,1,0:T(8,128)(2,1)} %get-tuple-element.9.sh_ref, f32[8,16,256]{2,1,0:T(8,128)} %get-tuple-element.10.meta_ref, bf16[256,2048]{1,0:T(8,128)(2,1)} %x_ref.3, bf16[8,1408,2048]{2,1,0:T(8,128)(2,1)} %w2_ref.1, ...), custom_call_target="tpu_custom_call" | custom-call | tf_op jit(solution)/shard_map/pallas_call | solution.py:549
  165.6 2.3 %copy.11 = bf16[256,2048]{1,0:T(8,128)(2,1)} copy(bf16[256,2048]{1,0:T(8,128)(2,1)} %shard_map.92) | data formatting | bytes 2097152

commit v7 on v6

--- a/solution.py
+++ b/solution.py
@@ -385,53 +385,6 @@
         s = core * 4 + chip[ch]
         return jnp.dot(wcv[s], o3[s], preferred_element_type=F32)
 
-    def compute(c):
-        def expert(e, _):
-            b = c * per + e
-            fetch(b + NW - 1)
-
-            @pl.when(c == 0)
-            def _():
-                hcopy(e).wait()
-            ready(b)
-            o = jnp.dot(hv[e], wb[lax.rem(b, NW)], preferred_element_type=F32).astype(BF)
-            for s in range(8):
-                for i in range(3):
-                    o3[s, pl.ds(pl.multiple_of(i * n + e * cap, 16), cap), :] = o[s * cap:(s + 1) * cap]
-            return 0
-
-        lax.fori_loop(0, el, expert, 0)
-
-        @pl.when(c == 0)
-        def _():
-            for d in loads:
-                d.start()
-
-        @pl.when(c >= 2)
-        def _():
-            for i in range(4):
-                swap(c - 2, i).wait_send()
-        for i, ch in enumerate("dxyo"):
-            give[lax.rem(c, 2), chip[ch]] = weigh(c, ch, 1 - ec)
-            swap(c, i).start()
-        for ch in "dxyo":
-            part[c, chip[ch]] = weigh(c, ch, ec)
-
-    def shared(c):
-        @pl.when(c == 0)
-        def _():
-            for d in loads:
-                d.wait()
-        s = None
-        for i in range(2):
-            b = c * per + el + i
-            fetch(b + NW - 1)
-            ready(b)
-            p = jnp.dot(shv[i], wb[lax.rem(b, NW)], preferred_element_type=F32)
-            s = p if s is None else s + p
-        cols = pl.ds(pl.multiple_of(c * CW, CW), CW)
-        res[c] = xv[:, cols].astype(F32) + s.astype(BF).astype(F32)
-
     def stage1(c):
         d, x, y, o = (chip[ch] for ch in "dxyo")
         swap(c, 0).wait_recv()
@@ -450,6 +403,65 @@
         sb[1, into, 2] = part[c, chip["y"], 0:half] + rv[0, c, 0]
         sb[0, into, 2] = part[c, chip["x"], half:t] + rv[1, c, 0]
 
+    def send(c):
+        @pl.when(c >= 2)
+        def _():
+            dispatch(c - 2, lambda d: d.wait_recv())
+            stage2(c - 2, c)
+        stage1(c)
+        dispatch(c, lambda d: d.start())
+
+    def compute(c):
+        def expert(e, _):
+            b = c * per + e
+            fetch(b + NW - 1)
+
+            @pl.when(c == 0)
+            def _():
+                hcopy(e).wait()
+            ready(b)
+            o = jnp.dot(hv[e], wb[lax.rem(b, NW)], preferred_element_type=F32).astype(BF)
+            for s in range(8):
+                for i in range(3):
+                    o3[s, pl.ds(pl.multiple_of(i * n + e * cap, 16), cap), :] = o[s * cap:(s + 1) * cap]
+            return 0
+
+        lax.fori_loop(0, el, expert, 0)
+
+        @pl.when(c >= 2)
+        def _():
+            send(c - 1)
+
+        @pl.when(c == 0)
+        def _():
+            for d in loads:
+                d.start()
+
+        @pl.when(c >= 2)
+        def _():
+            for i in range(4):
+                swap(c - 2, i).wait_send()
+        for i, ch in enumerate("dxyo"):
+            give[lax.rem(c, 2), chip[ch]] = weigh(c, ch, 1 - ec)
+            swap(c, i).start()
+        for ch in "dxyo":
+            part[c, chip[ch]] = weigh(c, ch, ec)
+
+    def shared(c):
+        @pl.when(c == 0)
+        def _():
+            for d in loads:
+                d.wait()
+        s = None
+        for i in range(2):
+            b = c * per + el + i
+            fetch(b + NW - 1)
+            ready(b)
+            p = jnp.dot(shv[i], wb[lax.rem(b, NW)], preferred_element_type=F32)
+            s = p if s is None else s + p
+        cols = pl.ds(pl.multiple_of(c * CW, CW), CW)
+        res[c] = xv[:, cols].astype(F32) + s.astype(BF).astype(F32)
+
     def ycopy(c):
         cols = pl.ds(pl.multiple_of(c * CW, CW), CW)
         return pltpu.make_async_copy(yst.at[lax.rem(c, 2)], y_ref.at[:, cols], ysem.at[lax.rem(c, 2)])
@@ -468,25 +480,24 @@
     def step(c, _):
         compute(c)
 
-        @pl.when(c >= 2)
-        def _():
-            dispatch(c - 2, lambda d: d.wait_recv())
-            stage2(c - 2, c)
-        stage1(c)
-        dispatch(c, lambda d: d.start())
+        @pl.when(c == 0)
+        def _():
+            send(0)
+        shared(c)
 
         @pl.when(c == nc - 1)
         def _():
+            send(nc - 1)
             for i in range(2):
                 ship(nc - 1, i, 1, 3, 0).start()
-        shared(c)
-
-        @pl.when(c >= 4)
-        def _():
-            stage3(c - 4)
+
+        @pl.when(c >= 5)
+        def _():
+            stage3(c - 5)
         return 0
 
     lax.fori_loop(0, nc, step, 0)
+    stage3(nc - 5)
     for i in range(2):
         ship(nc - 2, i, 0, 3).wait_recv()
     stage2(nc - 2, 0)

time: 168 us -> 172 us (1.024)
  Pallas kernels: 166 us -> 170 us
    pallas_call x1, Pallas kernels: 91 us -> 95.4 us  [local(): pl.pallas_call(functools.partial(second, el, cap), out_shape=jax.ShapeDty...]
where the time goes in v7:
time: 172 us
  Pallas kernels  170 us (99%)
  local copies, waits for them, and re-layouts  2.3 us (1%)
    pallas_call x1, Pallas kernels, local(): pl.pallas_call(functools.partial(second, el, cap), out_shape=jax.ShapeDty...  95.4 us
    pallas_call x1, Pallas kernels, local(): pl.pallas_call(functools.partial(first, el, cap), out_shape=(jax.ShapeDty...  74.6 us

profile of v7, /device:TPU:0, one launch (start us, length us, event | category | flops | bytes accessed | tf_op | source)
XLA Modules:
  0.0 172.3 jit_solution(3194512022634016817)
XLA Ops:
  0.0 74.6 %shard_map.91 = (bf16[8,384,1408]{2,1,0:T(8,128)(2,1)}, bf16[2,256,1408]{2,1,0:T(8,128)(2,1)}, f32[8,16,256]{2,1,0:T(8,128)}) custom-call(s32[6,256]{1,0:T(8,128)} %bitcast.2, f32[6,256]{1,0:T(8,128)} %bitcast.3, bf16[256,2048]{1,0:T(8,128)(2,1)} %x_ref.3, bf16[8,2048,1408]{2,1,0:T(8,128)(2,1)} %w1_ref.1, bf16[8,2048,1408]{2,1,0:T(8,128)(2,1)} %w3_ref.1, ...), custom_call_target="tpu_custom_call" | custom-call | tf_op jit(solution)/shard_map/pallas_call | solution.py:548
  74.6 95.4 %shard_map.92 = bf16[256,2048]{1,0:T(8,128)(2,1)} custom-call(bf16[8,384,1408]{2,1,0:T(8,128)(2,1)} %get-tuple-element.8.h_ref, bf16[2,256,1408]{2,1,0:T(8,128)(2,1)} %get-tuple-element.9.sh_ref, f32[8,16,256]{2,1,0:T(8,128)} %get-tuple-element.10.meta_ref, bf16[256,2048]{1,0:T(8,128)(2,1)} %x_ref.3, bf16[8,1408,2048]{2,1,0:T(8,128)(2,1)} %w2_ref.1, ...), custom_call_target="tpu_custom_call" | custom-call | tf_op jit(solution)/shard_map/pallas_call | solution.py:560
  170.0 2.3 %copy.11 = bf16[256,2048]{1,0:T(8,128)(2,1)} copy(bf16[256,2048]{1,0:T(8,128)(2,1)} %shard_map.92) | data formatting | bytes 2097152

commit v8 on v6

--- a/solution.py
+++ b/solution.py
@@ -300,16 +300,17 @@
 
 
 def second(el, cap, h_ref, sh_ref, meta_ref, x_ref, w2_ref, ws2_ref, y_ref,
-           hv, shv, wcv, meta, xv, wb, o3, part, give, pr, sb, rv, res, yst,
-           hsem, csem, xsem, wsem, ysem, psend, precv, ssem, rsem, esend, erecv):
+           hv, shv, wcv, meta, xv, wb, wd, o3, part, give, pr, sb, rv, res, yst,
+           hsem, csem, xsem, wsem, dsem, ysem, psend, precv, ssem, rsem, esend, erecv):
     ey, ex, ec, dev, chip = place()
     t, hd = x_ref.shape
     nc = hd // CW
     f = w2_ref.shape[1]
     half = t // 2
     lo, hi = pl.ds(0, half), pl.ds(half, half)
-    per = el + 2
+    per = el
     nb = nc * per
+    f = w2_ref.shape[1]
     n = el * cap
 
     def block(b, go):
@@ -317,14 +318,13 @@
         cols = pl.ds(pl.multiple_of(c * CW, CW), CW)
         slot = lax.rem(b, NW)
 
-        @pl.when((j < el) & (b < nb))
+        @pl.when(b < nb)
         def _():
             go(pltpu.make_async_copy(w2_ref.at[j, :, cols], wb.at[slot], wsem.at[slot]))
 
-        @pl.when((j >= el) & (b < nb))
-        def _():
-            rows = pl.ds(pl.multiple_of((j - el) * f, 128), f)
-            go(pltpu.make_async_copy(ws2_ref.at[rows, cols], wb.at[slot], wsem.at[slot]))
+    def down(c):
+        cols = pl.ds(pl.multiple_of(c * CW, CW), CW)
+        return pltpu.make_async_copy(ws2_ref.at[:, cols], wd.at[lax.rem(c, 2)], dsem.at[lax.rem(c, 2)])
 
     def fetch(b):
         block(b, lambda c: c.start())
@@ -336,7 +336,7 @@
         return pltpu.make_async_copy(h_ref.at[e], hv.at[e], hsem.at[e])
 
     hcopy(0).start()
-    for b in range(NW - 1):
+    for b in range(NW):
         fetch(b)
     for e in range(1, el):
         hcopy(e).start()
@@ -386,25 +386,26 @@
         return jnp.dot(wcv[s], o3[s], preferred_element_type=F32)
 
     def compute(c):
-        def expert(e, _):
-            b = c * per + e
-            fetch(b + NW - 1)
-
-            @pl.when(c == 0)
-            def _():
-                hcopy(e).wait()
-            ready(b)
-            o = jnp.dot(hv[e], wb[lax.rem(b, NW)], preferred_element_type=F32).astype(BF)
-            for s in range(8):
-                for i in range(3):
-                    o3[s, pl.ds(pl.multiple_of(i * n + e * cap, 16), cap), :] = o[s * cap:(s + 1) * cap]
+        def expert(i, _):
+            for e in (2 * i, 2 * i + 1):
+                @pl.when(c == 0)
+                def _():
+                    hcopy(e).wait()
+                ready(c * per + e)
+            for e in (2 * i, 2 * i + 1):
+                o = jnp.dot(hv[e], wb[lax.rem(c * per + e, NW)], preferred_element_type=F32).astype(BF)
+                for s in range(8):
+                    for j in range(3):
+                        o3[s, pl.ds(pl.multiple_of(j * n + e * cap, 16), cap), :] = o[s * cap:(s + 1) * cap]
+            for e in (2 * i, 2 * i + 1):
+                fetch(c * per + e + NW)
             return 0
 
-        lax.fori_loop(0, el, expert, 0)
-
-        @pl.when(c == 0)
-        def _():
-            for d in loads:
+        lax.fori_loop(0, el // 2, expert, 0)
+
+        @pl.when(c == 1)
+        def _():
+            for d in loads + [down(0), down(1)]:
                 d.start()
 
         @pl.when(c >= 2)
@@ -418,19 +419,11 @@
             part[c, chip[ch]] = weigh(c, ch, ec)
 
     def shared(c):
-        @pl.when(c == 0)
-        def _():
-            for d in loads:
-                d.wait()
-        s = None
-        for i in range(2):
-            b = c * per + el + i
-            fetch(b + NW - 1)
-            ready(b)
-            p = jnp.dot(shv[i], wb[lax.rem(b, NW)], preferred_element_type=F32)
-            s = p if s is None else s + p
+        down(c).wait()
+        p = [jnp.dot(shv[i], wd[lax.rem(c, 2), i * f:(i + 1) * f], preferred_element_type=F32) for i in range(2)]
         cols = pl.ds(pl.multiple_of(c * CW, CW), CW)
-        res[c] = xv[:, cols].astype(F32) + s.astype(BF).astype(F32)
+        res[c] = xv[:, cols].astype(F32) + (p[0] + p[1]).astype(BF).astype(F32)
+        pl.when(c + 2 < nc)(lambda: down(c + 2).start())
 
     def stage1(c):
         d, x, y, o = (chip[ch] for ch in "dxyo")
@@ -479,7 +472,14 @@
         def _():
             for i in range(2):
                 ship(nc - 1, i, 1, 3, 0).start()
-        shared(c)
+        @pl.when(c == 2)
+        def _():
+            for d in loads:
+                d.wait()
+
+        @pl.when(c >= 2)
+        def _():
+            shared(c - 2)
 
         @pl.when(c >= 4)
         def _():
@@ -487,6 +487,7 @@
         return 0
 
     lax.fori_loop(0, nc, step, 0)
+    lax.fori_loop(nc - 2, nc, lambda c, v: (shared(c), v)[1], 0)
     for i in range(2):
         ship(nc - 2, i, 0, 3).wait_recv()
     stage2(nc - 2, 0)
@@ -552,11 +553,11 @@
             in_specs=[ANY] * 6, out_specs=ANY,
             scratch_shapes=[
                 pltpu.VMEM((el, pg * cap, f), BF), pltpu.VMEM((2, t, f), BF), pltpu.VMEM((pg, t, 3 * n), BF), pltpu.VMEM((pg, 2 * el, t), F32),
-                pltpu.VMEM((t, hd), BF), pltpu.VMEM((NW, f, CW), BF), pltpu.VMEM((pg, 3 * n, CW), BF),
+                pltpu.VMEM((t, hd), BF), pltpu.VMEM((NW, f, CW), BF), pltpu.VMEM((2, 2 * f, CW), BF), pltpu.VMEM((pg, 3 * n, CW), BF),
                 pltpu.VMEM((nc, 4, t, CW), F32), pltpu.VMEM((2, 4, t, CW), F32), pltpu.VMEM((nc, 4, t, CW), F32),
                 pltpu.VMEM((2, nc, 3, t // 2, CW), F32), pltpu.VMEM((2, nc, 3, t // 2, CW), F32),
                 pltpu.VMEM((nc, t, CW), F32), pltpu.VMEM((2, t, CW), BF),
-                dma((el,)), dma, dma((2,)), dma((NW,)), dma((2,)), dma((nc, 4)), dma((nc, 4)), dma((nc, 2)), dma((nc, 2)),
+                dma((el,)), dma, dma((2,)), dma((NW,)), dma((2,)), dma((2,)), dma((nc, 4)), dma((nc, 4)), dma((nc, 2)), dma((nc, 2)),
                 dma((3, 2)), dma((3, 2))],
             compiler_params=pltpu.CompilerParams(collective_id=1, has_side_effects=True, vmem_limit_bytes=VLIM),
         )(h, sh, meta, x, w2, ws2)

time: 168 us -> 165 us (0.982)
  Pallas kernels: 166 us -> 162 us
    pallas_call x1, Pallas kernels: 91 us -> 87.4 us  [local(): pl.pallas_call(functools.partial(second, el, cap), out_shape=jax.ShapeDty...]
where the time goes in v8:
time: 165 us; the launch traced here: 164 us
  Pallas kernels  162 us (98%)
  local copies, waits for them, and re-layouts  2.3 us (1%)
    pallas_call x1, Pallas kernels, local(): pl.pallas_call(functools.partial(second, el, cap), out_shape=jax.ShapeDty...  87.4 us
    pallas_call x1, Pallas kernels, local(): pl.pallas_call(functools.partial(first, el, cap), out_shape=(jax.ShapeDty...  74.6 us

profile of v8, /device:TPU:0, one launch (start us, length us, event | category | flops | bytes accessed | tf_op | source)
XLA Modules:
  0.0 164.3 jit_solution(8065787712823262387)
XLA Ops:
  0.0 74.6 %shard_map.91 = (bf16[8,384,1408]{2,1,0:T(8,128)(2,1)}, bf16[2,256,1408]{2,1,0:T(8,128)(2,1)}, f32[8,16,256]{2,1,0:T(8,128)}) custom-call(s32[6,256]{1,0:T(8,128)} %bitcast.2, f32[6,256]{1,0:T(8,128)} %bitcast.3, bf16[256,2048]{1,0:T(8,128)(2,1)} %x_ref.3, bf16[8,2048,1408]{2,1,0:T(8,128)(2,1)} %w1_ref.1, bf16[8,2048,1408]{2,1,0:T(8,128)(2,1)} %w3_ref.1, ...), custom_call_target="tpu_custom_call" | custom-call | tf_op jit(solution)/shard_map/pallas_call | solution.py:538
  74.6 87.4 %shard_map.92 = bf16[256,2048]{1,0:T(8,128)(2,1)} custom-call(bf16[8,384,1408]{2,1,0:T(8,128)(2,1)} %get-tuple-element.8.h_ref, bf16[2,256,1408]{2,1,0:T(8,128)(2,1)} %get-tuple-element.9.sh_ref, f32[8,16,256]{2,1,0:T(8,128)} %get-tuple-element.10.meta_ref, bf16[256,2048]{1,0:T(8,128)(2,1)} %x_ref.3, bf16[8,1408,2048]{2,1,0:T(8,128)(2,1)} %w2_ref.1, ...), custom_call_target="tpu_custom_call" | custom-call | tf_op jit(solution)/shard_map/pallas_call | solution.py:550
  162.0 2.3 %copy.11 = bf16[256,2048]{1,0:T(8,128)(2,1)} copy(bf16[256,2048]{1,0:T(8,128)(2,1)} %shard_map.92) | data formatting | bytes 2097152

commit v9 on v8

--- a/solution.py
+++ b/solution.py
@@ -77,10 +77,10 @@
         for j in range(2):
             ready(b + j)
 
+    for k in range(NK):
+        pltpu.make_async_copy(x_ref.at[:, pl.ds(k * kw, kw)], xg.at[k, mine["o"]], xsem.at[k]).start()
     for b in range(NS - 2):
         fetch(b)
-    for k in range(NK):
-        pltpu.make_async_copy(x_ref.at[:, pl.ds(k * kw, kw)], xg.at[k, mine["o"]], xsem.at[k]).start()
 
     ne = el * 8
     row = lax.broadcasted_iota(jnp.int32, (ne, t), 0)
@@ -117,18 +117,20 @@
                                             device_id_type=MESH)
 
     def direct(k):
-        for chan, to in enumerate("xyp"):
-            remote(k, mine["o"], full, chan, to).start()
+        for rows, chan, to in ((lo, 0, "x"), (hi, 1, "y"), (hi, 9, "x"), (lo, 10, "y"), (full, 2, "p")):
+            remote(k, mine["o"], rows, chan, to).start()
 
     def relay(k):
-        remote(k, mine["x"], full, 0, "x").wait_recv()
+        remote(k, mine["x"], lo, 0, "x").wait_recv()
         remote(k, mine["x"], lo, 3, "y").start()
+        remote(k, mine["y"], hi, 1, "y").wait_recv()
+        remote(k, mine["y"], hi, 4, "x").start()
+
+    def corner(k):
+        remote(k, mine["x"], hi, 9, "x").wait_recv()
         remote(k, mine["x"], full, 5, "p").start()
-        remote(k, mine["y"], full, 1, "y").wait_recv()
-        remote(k, mine["y"], hi, 4, "x").start()
+        remote(k, mine["y"], lo, 10, "y").wait_recv()
         remote(k, mine["y"], full, 6, "p").start()
-
-    def corner(k):
         remote(k, mine["d"], lo, 3, "y").wait_recv()
         remote(k, mine["d"], lo, 7, "p").start()
         remote(k, mine["d"], hi, 4, "x").wait_recv()
@@ -142,7 +144,8 @@
         remote(k, theirs["d"], hi, 8, "p").wait_recv()
 
     def sent(k):
-        for src, rows, chan, to in ((mine["o"], full, 0, "x"), (mine["o"], full, 1, "y"), (mine["o"], full, 2, "p"),
+        for src, rows, chan, to in ((mine["o"], lo, 0, "x"), (mine["o"], hi, 9, "x"), (mine["o"], hi, 1, "y"),
+                                    (mine["o"], lo, 10, "y"), (mine["o"], full, 2, "p"),
                                     (mine["x"], lo, 3, "y"), (mine["y"], hi, 4, "x"), (mine["x"], full, 5, "p"),
                                     (mine["y"], full, 6, "p"), (mine["d"], lo, 7, "p"), (mine["d"], hi, 8, "p")):
             remote(k, src, rows, chan, to).wait_send()
@@ -335,6 +338,8 @@
     def hcopy(e):
         return pltpu.make_async_copy(h_ref.at[e], hv.at[e], hsem.at[e])
 
+    m = pltpu.make_async_copy(meta_ref, meta, csem)
+    m.start()
     hcopy(0).start()
     for b in range(NW):
         fetch(b)
@@ -342,8 +347,6 @@
         hcopy(e).start()
     loads = [pltpu.make_async_copy(sh_ref, shv, xsem.at[0]), pltpu.make_async_copy(x_ref, xv, xsem.at[1]),
              ]
-    m = pltpu.make_async_copy(meta_ref, meta, csem)
-    m.start()
 
     barrier = pltpu.get_barrier_semaphore()
     for to in "xyp":
@@ -544,7 +547,7 @@
                 pltpu.VMEM((NK, pg, t, kw), BF), pltpu.VMEM((el, pg * cap, 2 * f), F32), pltpu.VMEM((NS, kw, 2 * f), BF),
                 pltpu.VMEM((pg, n, t), BF), pltpu.VMEM((el, pg, cap, kw), BF), pltpu.VMEM((2, pg * cap, f), BF),
                 pltpu.VMEM((pg, 2 * el, t), F32), pltpu.VMEM((pg, 2 * el, t), F32),
-                dma((NK,)), dma((NS, 2)), dma((2,)), dma, dma((8,)), dma((8,)), dma((NK, 9)), dma((NK, 9))],
+                dma((NK,)), dma((NS, 2)), dma((2,)), dma, dma((8,)), dma((8,)), dma((NK, 11)), dma((NK, 11))],
             compiler_params=pltpu.CompilerParams(collective_id=0, has_side_effects=True, vmem_limit_bytes=VLIM),
         )(ids.T, gates.T, x, w1, w3, ws1, ws3)
         return pl.pallas_call(

time: 165 us -> 162 us (0.982)
  Pallas kernels: 162 us -> 160 us
where the time goes in v9:
time: 162 us
  Pallas kernels  160 us (99%)
  local copies, waits for them, and re-layouts  2.3 us (1%)
    pallas_call x1, Pallas kernels, local(): pl.pallas_call(functools.partial(second, el, cap), out_shape=jax.ShapeDty...  86.2 us
    pallas_call x1, Pallas kernels, local(): pl.pallas_call(functools.partial(first, el, cap), out_shape=(jax.ShapeDty...  73.4 us

profile of v9, /device:TPU:0, one launch (start us, length us, event | category | flops | bytes accessed | tf_op | source)
XLA Modules:
  0.0 162.0 jit_solution(2394702602371538762)
XLA Ops:
  0.0 73.4 %shard_map.91 = (bf16[8,384,1408]{2,1,0:T(8,128)(2,1)}, bf16[2,256,1408]{2,1,0:T(8,128)(2,1)}, f32[8,16,256]{2,1,0:T(8,128)}) custom-call(s32[6,256]{1,0:T(8,128)} %bitcast.2, f32[6,256]{1,0:T(8,128)} %bitcast.3, bf16[256,2048]{1,0:T(8,128)(2,1)} %x_ref.3, bf16[8,2048,1408]{2,1,0:T(8,128)(2,1)} %w1_ref.1, bf16[8,2048,1408]{2,1,0:T(8,128)(2,1)} %w3_ref.1, ...), custom_call_target="tpu_custom_call" | custom-call | tf_op jit(solution)/shard_map/pallas_call | solution.py:541
  73.5 86.2 %shard_map.92 = bf16[256,2048]{1,0:T(8,128)(2,1)} custom-call(bf16[8,384,1408]{2,1,0:T(8,128)(2,1)} %get-tuple-element.8.h_ref, bf16[2,256,1408]{2,1,0:T(8,128)(2,1)} %get-tuple-element.9.sh_ref, f32[8,16,256]{2,1,0:T(8,128)} %get-tuple-element.10.meta_ref, bf16[256,2048]{1,0:T(8,128)(2,1)} %x_ref.3, bf16[8,1408,2048]{2,1,0:T(8,128)(2,1)} %w2_ref.1, ...), custom_call_target="tpu_custom_call" | custom-call | tf_op jit(solution)/shard_map/pallas_call | solution.py:553
  159.7 2.3 %copy.11 = bf16[256,2048]{1,0:T(8,128)(2,1)} copy(bf16[256,2048]{1,0:T(8,128)(2,1)} %shard_map.92) | data formatting | bytes 2097152

commit v10 on v9

--- a/solution.py
+++ b/solution.py
@@ -73,13 +73,11 @@
 
     def pair(b):
         for j in range(2):
-            fetch(b + NS - 2 + j)
-        for j in range(2):
             ready(b + j)
 
     for k in range(NK):
         pltpu.make_async_copy(x_ref.at[:, pl.ds(k * kw, kw)], xg.at[k, mine["o"]], xsem.at[k]).start()
-    for b in range(NS - 2):
+    for b in range(NS):
         fetch(b)
 
     ne = el * 8
@@ -172,6 +170,8 @@
                 d = [jnp.dot(xg[2 * i + j, mine["o"]], wb[lax.rem(b + j, NS), :, at], preferred_element_type=F32)
                      for j in range(2)]
                 acc[0, 0:t, at] += d[0] + d[1]
+            for j in range(2):
+                fetch(b + NS + j)
             return 0
 
         lax.fori_loop(0, NK // 2, body, 0)
@@ -214,6 +214,7 @@
             slot = lax.rem(b + j, NS)
             u = xe[2 * i + j].reshape(8 * cap, kw)
             use(2 * i + j, lambda at, u=u, slot=slot: jnp.dot(u, wb[slot, :, at], preferred_element_type=F32))
+            fetch(b + j + NS)
 
     def slabs(w):
         return [slice(i, min(i + w, 2 * f)) for i in range(0, 2 * f, w)]
@@ -228,10 +229,9 @@
     corner(0)
     arrived(0)
     gather(0)
-    lax.fori_loop(0, el // 8, start_acc, 0)
     relay(1)
     direct(2)
-    lax.fori_loop(el // 8, el // 2 - el // 8, start_acc, 0)
+    lax.fori_loop(0, el // 2 - el // 8, start_acc, 0)
     corner(1)
     lax.fori_loop(el // 2 - el // 8, el // 2, start_acc, 0)
 
@@ -246,13 +246,12 @@
             products(k, i, use)
             return 0
 
-        lax.fori_loop(0, el // 8, add, 0)
         relay(k + 1)
 
         @pl.when(k < NK - 2)
         def _():
             direct(k + 2)
-        lax.fori_loop(el // 8, el // 2 - el // 8, add, 0)
+        lax.fori_loop(0, el // 2 - el // 8, add, 0)
         corner(k + 1)
         lax.fori_loop(el // 2 - el // 8, el // 2, add, 0)
         return 0
@@ -429,7 +428,7 @@
         pl.when(c + 2 < nc)(lambda: down(c + 2).start())
 
     def stage1(c):
-        d, x, y, o = (chip[ch] for ch in "dxyo")
+        d, x, y = (chip[ch] for ch in "dxy")
         swap(c, 0).wait_recv()
         sb[0, c, 0] = part[c, d, 0:half] + pr[c, d, 0:half]
         sb[1, c, 0] = part[c, d, half:t] + pr[c, d, half:t]
@@ -439,8 +438,6 @@
         swap(c, 2).wait_recv()
         part[c, y, 0:half] += pr[c, y, 0:half]
         sb[1, c, 1] = part[c, y, half:t] + pr[c, y, half:t]
-        swap(c, 3).wait_recv()
-        part[c, o] += pr[c, o]
 
     def stage2(c, into):
         sb[1, into, 2] = part[c, chip["y"], 0:half] + rv[0, c, 0]
@@ -456,7 +453,8 @@
         @pl.when(c >= 2)
         def _():
             ycopy(c - 2).wait()
-        own = res[c] + part[c, chip["o"]]
+        swap(c, 3).wait_recv()
+        own = res[c] + (part[c, chip["o"]] + pr[c, chip["o"]])
         yst[lax.rem(c, 2), 0:half] = (own[0:half] + rv[0, c, 1] + rv[1, n2, 2]).astype(BF)
         yst[lax.rem(c, 2), half:t] = (own[half:t] + rv[0, n2, 2] + rv[1, c, 1]).astype(BF)
         ycopy(c).start()

time: 162 us -> 163 us (level)
  no operation moved by 1% of the time
where the time goes in v10:
time: 163 us
  Pallas kernels  160 us (98%)
  local copies, waits for them, and re-layouts  2.3 us (1%)
    pallas_call x1, Pallas kernels, local(): pl.pallas_call(functools.partial(second, el, cap), out_shape=jax.ShapeDty...  85.7 us
    pallas_call x1, Pallas kernels, local(): pl.pallas_call(functools.partial(first, el, cap), out_shape=(jax.ShapeDty...  74.5 us

profile of v10, /device:TPU:0, one launch (start us, length us, event | category | flops | bytes accessed | tf_op | source)
XLA Modules:
  0.0 162.5 jit_solution(7052080053154321301)
XLA Ops:
  0.0 74.5 %shard_map.91 = (bf16[8,384,1408]{2,1,0:T(8,128)(2,1)}, bf16[2,256,1408]{2,1,0:T(8,128)(2,1)}, f32[8,16,256]{2,1,0:T(8,128)}) custom-call(s32[6,256]{1,0:T(8,128)} %bitcast.2, f32[6,256]{1,0:T(8,128)} %bitcast.3, bf16[256,2048]{1,0:T(8,128)(2,1)} %x_ref.3, bf16[8,2048,1408]{2,1,0:T(8,128)(2,1)} %w1_ref.1, bf16[8,2048,1408]{2,1,0:T(8,128)(2,1)} %w3_ref.1, ...), custom_call_target="tpu_custom_call" | custom-call | tf_op jit(solution)/shard_map/pallas_call | solution.py:539
  74.5 85.7 %shard_map.92 = bf16[256,2048]{1,0:T(8,128)(2,1)} custom-call(bf16[8,384,1408]{2,1,0:T(8,128)(2,1)} %get-tuple-element.8.h_ref, bf16[2,256,1408]{2,1,0:T(8,128)(2,1)} %get-tuple-element.9.sh_ref, f32[8,16,256]{2,1,0:T(8,128)} %get-tuple-element.10.meta_ref, bf16[256,2048]{1,0:T(8,128)(2,1)} %x_ref.3, bf16[8,1408,2048]{2,1,0:T(8,128)(2,1)} %w2_ref.1, ...), custom_call_target="tpu_custom_call" | custom-call | tf_op jit(solution)/shard_map/pallas_call | solution.py:551
  160.2 2.3 %copy.11 = bf16[256,2048]{1,0:T(8,128)(2,1)} copy(bf16[256,2048]{1,0:T(8,128)(2,1)} %shard_map.92) | data formatting | bytes 2097152

commit v11 on v9

--- a/solution.py
+++ b/solution.py
@@ -429,7 +429,7 @@
         pl.when(c + 2 < nc)(lambda: down(c + 2).start())
 
     def stage1(c):
-        d, x, y, o = (chip[ch] for ch in "dxyo")
+        d, x, y = (chip[ch] for ch in "dxy")
         swap(c, 0).wait_recv()
         sb[0, c, 0] = part[c, d, 0:half] + pr[c, d, 0:half]
         sb[1, c, 0] = part[c, d, half:t] + pr[c, d, half:t]
@@ -439,8 +439,6 @@
         swap(c, 2).wait_recv()
         part[c, y, 0:half] += pr[c, y, 0:half]
         sb[1, c, 1] = part[c, y, half:t] + pr[c, y, half:t]
-        swap(c, 3).wait_recv()
-        part[c, o] += pr[c, o]
 
     def stage2(c, into):
         sb[1, into, 2] = part[c, chip["y"], 0:half] + rv[0, c, 0]
@@ -456,7 +454,8 @@
         @pl.when(c >= 2)
         def _():
             ycopy(c - 2).wait()
-        own = res[c] + part[c, chip["o"]]
+        swap(c, 3).wait_recv()
+        own = res[c] + (part[c, chip["o"]] + pr[c, chip["o"]])
         yst[lax.rem(c, 2), 0:half] = (own[0:half] + rv[0, c, 1] + rv[1, n2, 2]).astype(BF)
         yst[lax.rem(c, 2), half:t] = (own[half:t] + rv[0, n2, 2] + rv[1, c, 1]).astype(BF)
         ycopy(c).start()

time: 162 us -> 161 us (level)
  no operation moved by 1% of the time
where the time goes in v11:
time: 161 us
  Pallas kernels  159 us (99%)
  local copies, waits for them, and re-layouts  2.3 us (1%)
    pallas_call x1, Pallas kernels, local(): pl.pallas_call(functools.partial(second, el, cap), out_shape=jax.ShapeDty...  85.3 us
    pallas_call x1, Pallas kernels, local(): pl.pallas_call(functools.partial(first, el, cap), out_shape=(jax.ShapeDty...  73.4 us

profile of v11, /device:TPU:0, one launch (start us, length us, event | category | flops | bytes accessed | tf_op | source)
XLA Modules:
  0.0 161.1 jit_solution(16163358710027699184)
XLA Ops:
  0.0 73.4 %shard_map.91 = (bf16[8,384,1408]{2,1,0:T(8,128)(2,1)}, bf16[2,256,1408]{2,1,0:T(8,128)(2,1)}, f32[8,16,256]{2,1,0:T(8,128)}) custom-call(s32[6,256]{1,0:T(8,128)} %bitcast.2, f32[6,256]{1,0:T(8,128)} %bitcast.3, bf16[256,2048]{1,0:T(8,128)(2,1)} %x_ref.3, bf16[8,2048,1408]{2,1,0:T(8,128)(2,1)} %w1_ref.1, bf16[8,2048,1408]{2,1,0:T(8,128)(2,1)} %w3_ref.1, ...), custom_call_target="tpu_custom_call" | custom-call | tf_op jit(solution)/shard_map/pallas_call | solution.py:540
  73.5 85.3 %shard_map.92 = bf16[256,2048]{1,0:T(8,128)(2,1)} custom-call(bf16[8,384,1408]{2,1,0:T(8,128)(2,1)} %get-tuple-element.8.h_ref, bf16[2,256,1408]{2,1,0:T(8,128)(2,1)} %get-tuple-element.9.sh_ref, f32[8,16,256]{2,1,0:T(8,128)} %get-tuple-element.10.meta_ref, bf16[256,2048]{1,0:T(8,128)(2,1)} %x_ref.3, bf16[8,1408,2048]{2,1,0:T(8,128)(2,1)} %w2_ref.1, ...), custom_call_target="tpu_custom_call" | custom-call | tf_op jit(solution)/shard_map/pallas_call | solution.py:552
  158.8 2.3 %copy.11 = bf16[256,2048]{1,0:T(8,128)(2,1)} copy(bf16[256,2048]{1,0:T(8,128)(2,1)} %shard_map.92) | data formatting | bytes 2097152

commit v12 on v11

--- a/solution.py
+++ b/solution.py
@@ -82,6 +82,15 @@
     for b in range(NS - 2):
         fetch(b)
 
+    barrier = pltpu.get_barrier_semaphore()
+    others = [(a, b, c) for a in (0, 1) for b in (0, 1) for c in (0, 1) if a + b + c]
+
+    def flip(o):
+        return [lax.rem(v + s, 2) for v, s in zip((ey, ex, ec), o)]
+
+    for o in others:
+        y2, x2, c2 = flip(o)
+        pl.semaphore_signal(barrier, inc=1, device_id=dict(ey=y2, ex=x2, ec=c2), device_id_type=MESH)
     ne = el * 8
     row = lax.broadcasted_iota(jnp.int32, (ne, t), 0)
     chosen = jnp.zeros((ne, t), F32)
@@ -97,15 +106,6 @@
         mout[d, 0:el, :] = rank[d * el:(d + 1) * el]
         mout[d, el:2 * el, :] = gate[d * el:(d + 1) * el]
 
-    barrier = pltpu.get_barrier_semaphore()
-    others = [(a, b, c) for a in (0, 1) for b in (0, 1) for c in (0, 1) if a + b + c]
-
-    def flip(o):
-        return [lax.rem(v + s, 2) for v, s in zip((ey, ex, ec), o)]
-
-    for o in others:
-        y2, x2, c2 = flip(o)
-        pl.semaphore_signal(barrier, inc=1, device_id=dict(ey=y2, ex=x2, ec=c2), device_id_type=MESH)
     pl.semaphore_wait(barrier, len(others))
 
     for k in range(NK):
@@ -313,6 +313,7 @@
     lo, hi = pl.ds(0, half), pl.ds(half, half)
     per = el
     nb = nc * per
+    assert NW == el
     f = w2_ref.shape[1]
     n = el * cap
 
@@ -340,18 +341,15 @@
 
     m = pltpu.make_async_copy(meta_ref, meta, csem)
     m.start()
-    hcopy(0).start()
-    for b in range(NW):
-        fetch(b)
-    for e in range(1, el):
+    for e in range(el):
         hcopy(e).start()
+        fetch(e)
     loads = [pltpu.make_async_copy(sh_ref, shv, xsem.at[0]), pltpu.make_async_copy(x_ref, xv, xsem.at[1]),
              ]
 
     barrier = pltpu.get_barrier_semaphore()
     for to in "xyp":
         pl.semaphore_signal(barrier, inc=1, device_id=dev[to], device_id_type=MESH)
-    pl.semaphore_wait(barrier, 3)
 
     m.wait()
     slots = lax.broadcasted_iota(jnp.int32, (cap, t), 0).astype(F32)
@@ -366,6 +364,8 @@
         return 0
 
     lax.fori_loop(0, 8, build, 0)
+
+    pl.semaphore_wait(barrier, 3)
 
     def swap(c, i):
         ch = chip["dxyo"[i]]

time: 161 us -> 161 us (level)
  no operation moved by 1% of the time
where the time goes in v12:
time: 161 us
  Pallas kernels  159 us (99%)
  local copies, waits for them, and re-layouts  2.3 us (1%)
    pallas_call x1, Pallas kernels, local(): pl.pallas_call(functools.partial(second, el, cap), out_shape=jax.ShapeDty...  85.3 us
    pallas_call x1, Pallas kernels, local(): pl.pallas_call(functools.partial(first, el, cap), out_shape=(jax.ShapeDty...  73.5 us

profile of v12, /device:TPU:0, one launch (start us, length us, event | category | flops | bytes accessed | tf_op | source)
XLA Modules:
  0.0 161.2 jit_solution(6029788622708327395)
XLA Ops:
  0.0 73.5 %shard_map.91 = (bf16[8,384,1408]{2,1,0:T(8,128)(2,1)}, bf16[2,256,1408]{2,1,0:T(8,128)(2,1)}, f32[8,16,256]{2,1,0:T(8,128)}) custom-call(s32[6,256]{1,0:T(8,128)} %bitcast.2, f32[6,256]{1,0:T(8,128)} %bitcast.3, bf16[256,2048]{1,0:T(8,128)(2,1)} %x_ref.3, bf16[8,2048,1408]{2,1,0:T(8,128)(2,1)} %w1_ref.1, bf16[8,2048,1408]{2,1,0:T(8,128)(2,1)} %w3_ref.1, ...), custom_call_target="tpu_custom_call" | custom-call | tf_op jit(solution)/shard_map/pallas_call | solution.py:540
  73.5 85.3 %shard_map.92 = bf16[256,2048]{1,0:T(8,128)(2,1)} custom-call(bf16[8,384,1408]{2,1,0:T(8,128)(2,1)} %get-tuple-element.8.h_ref, bf16[2,256,1408]{2,1,0:T(8,128)(2,1)} %get-tuple-element.9.sh_ref, f32[8,16,256]{2,1,0:T(8,128)} %get-tuple-element.10.meta_ref, bf16[256,2048]{1,0:T(8,128)(2,1)} %x_ref.3, bf16[8,1408,2048]{2,1,0:T(8,128)(2,1)} %w2_ref.1, ...), custom_call_target="tpu_custom_call" | custom-call | tf_op jit(solution)/shard_map/pallas_call | solution.py:552
  158.8 2.3 %copy.11 = bf16[256,2048]{1,0:T(8,128)(2,1)} copy(bf16[256,2048]{1,0:T(8,128)(2,1)} %shard_map.92) | data formatting | bytes 2097152
